TPU v7x, 256 devices: a whole 4x4x8 slice. The times are simulated.
256 devices in a mesh: seq: 32 (over y, z), batch: 8 (over x, core).
Axes of the slice: x: 4, y: 4, z: 8, core: 2. Of those that a mesh axis runs over, the one named last changes fastest.
Arguments:
- conv_input: bfloat16 [32768, 8192], P(('batch', 'seq')), parts along dimension 0, may hold values from -6 to 6
- gate_input: bfloat16 [32768, 8192], P(('batch', 'seq')), parts along dimension 0, may hold values from -6 to 6
- conv_weight: bfloat16 [4, 8192], P(None, 'seq'), may hold values from -3 to 3
- conv_bias: bfloat16 [8192], P('seq'), may hold values from -3 to 3
- x_weight: bfloat16 [8192, 288], P('seq'), may hold values from -0.0625 to 0.0625
- dt_gain: float32 [256], replicated, may hold values from 0.5 to 1.5
- dt_weight: bfloat16 [256, 8192], P(None, 'seq'), may hold values from -0.375 to 0.375
- dt_bias: float32 [8192], P('seq'), may hold values from -6.9 to -2.3
- a_log: float32 [16, 8192], P(None, 'seq'), may hold values from 0 to 2.77
- skip: float32 [8192], P('seq'), may hold values from 0.5 to 1.5
Outputs:
- mixed: bfloat16 [32768, 8192], P(('batch', 'seq')), parts along dimension 0
There are 8 independent parts, one for each index of `batch`. A program takes and returns all parts, laid end to end along the dimension named above; an argument that names none is the same for every part. Nothing has to cross between parts.
All inputs are finite; a program needn't handle non-finite values.
Results may differ from a plain program's by a relative error of at most 0.0085.
Values may be sent and summed in bfloat16 or wider, within the bound.
A program may use at most 128 MiB of HBM per device.

v0:
```python
import jax
import jax.numpy as jnp
from jax import lax
from jax.sharding import PartitionSpec as P


def passed_along(value, axis, steps):
    count = lax.axis_size(axis)
    initial, last = (max(0, -steps), min(count, count - steps))
    return lax.ppermute(value, axis, [(source, source + steps) for source in range(initial, last)])


def from_everyone(x, axis):
    copies = jnp.broadcast_to(x, (lax.axis_size(axis), *x.shape))
    return lax.all_to_all(copies, axis, split_axis=0, concat_axis=0, tiled=True)


def joined_along(parts, dim):
    parts = jnp.moveaxis(parts, 0, dim)
    dims = parts.shape
    return parts.reshape(*dims[:dim], dims[dim] * dims[dim + 1], *dims[dim + 2 :])


def gather_directly(x, axis, dim):
    parts = from_everyone(x, axis)
    return joined_along(parts, dim)


def causal_conv(prefix, inputs, weight, bias):
    rows = inputs.shape[0]
    width = weight.shape[0]
    padded = jnp.concatenate([prefix, inputs.astype(jnp.float32)], 0)
    total = bias.astype(jnp.float32)[None, :]
    for tap in range(width):
        total = total + weight[tap].astype(jnp.float32)[None, :] * padded[tap : tap + rows]
    return jax.nn.silu(total).astype(jnp.bfloat16)


def link_blocks(earlier, later):
    return (earlier[0] * later[0], later[0] * earlier[1] + later[1])


def selective_scan(step, xfloat, bmat, cmat, rate):
    span = 16
    length, chans = step.shape
    states = rate.shape[0]
    blocks = length // span
    step_rows = step.reshape(blocks, span * chans)
    drive_rows = (step * xfloat).reshape(blocks, span * chans)
    b_rows = bmat.reshape(blocks, span * states)
    c_rows = cmat.reshape(blocks, span * states)
    state = jnp.zeros((blocks, states, chans), jnp.float32)
    running = jnp.zeros((blocks, chans), jnp.float32)
    local_parts = []
    elapsed = []
    for place in range(span):
        step_now = step_rows[:, place * chans : (place + 1) * chans]
        drive_now = drive_rows[:, place * chans : (place + 1) * chans]
        b_now = b_rows[:, place * states : (place + 1) * states]
        c_now = c_rows[:, place * states : (place + 1) * states]
        state = (
            jnp.exp(step_now[:, None, :] * rate[None]) * state
            + b_now[:, :, None] * drive_now[:, None, :]
        )
        local_parts.append(jnp.sum(c_now[:, :, None] * state, axis=1))
        running = running + step_now
        elapsed.append(running)
    totals = jnp.exp(running[:, None, :] * rate[None])
    _, through = lax.associative_scan(link_blocks, (totals, state), axis=0)
    starts = jnp.concatenate([jnp.zeros((1, states, chans), jnp.float32), through[: blocks - 1]], 0)
    pieces = []
    for place in range(span):
        c_now = c_rows[:, place * states : (place + 1) * states]
        carried = jnp.sum(
            c_now[:, :, None] * jnp.exp(elapsed[place][:, None, :] * rate[None]) * starts, axis=1
        )
        pieces.append(local_parts[place] + carried)
    return jnp.concatenate(pieces, 1).reshape(length, chans)


def local(
    conv_input,
    gate_input,
    conv_weight,
    conv_bias,
    x_weight,
    dt_gain,
    dt_weight,
    dt_bias,
    a_log,
    skip,
):
    width = conv_weight.shape[0]
    rank = dt_weight.shape[0]
    states = a_log.shape[0]
    prior = passed_along(conv_input[conv_input.shape[0] - (width - 1) :], "seq", 1)
    params = gather_directly(jnp.concatenate([conv_weight, conv_bias[None, :]], 0), "seq", 1)
    outgoing = causal_conv(prior.astype(jnp.float32), conv_input, params[:width], params[width])
    local_proj = jnp.dot(
        outgoing,
        lax.all_gather(x_weight, "seq", axis=0, tiled=True),
        preferred_element_type=jnp.float32,
    )
    arrived, gate_part = (
        lax.all_to_all(outgoing, "seq", split_axis=1, concat_axis=0, tiled=True),
        lax.all_to_all(gate_input, "seq", split_axis=1, concat_axis=0, tiled=True),
    )
    proj = lax.all_gather(local_proj, "seq", axis=0, tiled=True)
    dt_low = proj[:, :rank]
    bmat = proj[:, rank : rank + states]
    cmat = proj[:, rank + states :]
    normed = (
        dt_low
        * lax.rsqrt(jnp.mean(dt_low * dt_low, axis=1, keepdims=True) + 1e-06)
        * dt_gain[None, :]
    ).astype(jnp.bfloat16)
    step = jax.nn.softplus(
        jnp.dot(normed, dt_weight, preferred_element_type=jnp.float32) + dt_bias[None, :]
    )
    rate = -jnp.exp(a_log)
    xfloat = arrived.astype(jnp.float32)
    scanned = selective_scan(step, xfloat, bmat, cmat, rate)
    y_out = (scanned + skip[None, :] * xfloat).astype(jnp.bfloat16)
    held = lax.optimization_barrier(y_out)
    gated = (held.astype(jnp.float32) * jax.nn.silu(gate_part.astype(jnp.float32))).astype(
        jnp.bfloat16
    )
    return lax.all_to_all(gated, "seq", split_axis=0, concat_axis=1, tiled=True)


def solution(mesh):
    return jax.shard_map(
        local,
        mesh=mesh,
        in_specs=(
            P(("batch", "seq"), None),
            P(("batch", "seq"), None),
            P(None, "seq"),
            P("seq"),
            P("seq", None),
            P(),
            P(None, "seq"),
            P("seq"),
            P(None, "seq"),
            P("seq"),
        ),
        out_specs=P(("batch", "seq"), None),
        check_vma=False,
    )
```

profile of v0, /device:TPU:8, one launch (start us, length us, event | category | flops | bytes accessed | tf_op | source)
XLA Modules:
  0.0 657.6 jit_solution(11097169348318939079)
XLA Ops:
  9.3 11.7 %all-to-all-start = ((bf16[32,5,256]{2,1,0:T(8,128)(2,1)}), bf16[32,5,256]{2,1,0:T(8,128)(2,1)S(1)}, u32[]{:S(2)}, u32[]{:S(2)}) async-start(bf16[32,5,256]{2,1,0:T(8,128)(2,1)} %broadcast_in_dim.7), calls=%async_computation | async-start | bytes 262144 | tf_op jit(solution)/shard_map/all_to_all | solution.py:15
  22.0 3.4 collective-permute-start
  25.4 4.1 convert_element_type.94
  31.2 7.6 %multiply_convert_fusion.1 = bf16[128,8192]{1,0:T(8,128)(2,1)S(1)} fusion(f32[128,8192]{1,0:T(8,128)} %convert_element_type.94, f32[3,8192]{1,0:T(4,128)S(1)} %convert_element_type.93, f32[8192]{0:T(1024)S(1)} %bitcast.55, f32[8192]{0:T(1024)S(1)} %bitcast.56, f32[8192]{0:T(1024)S(1)} %bitcast.57, f32[8192]{0:T(1024)S(1)} %bitcast.58, f32[8192]{0:T(1024)S(1)} %bitcast.54), kind=kLoop, calls=%fused_computation.78 | loop fusion | flops 16777216 | bytes 6553600 | tf_op jit(solution)/shard_map/convert_element_type | solution.py:36
  38.8 58.9 %all-gather.3.cloned.1.call-done = bf16[8192,288]{0,1:T(8,128)(2,1)} async-done(((bf16[256,288]{0,1:T(8,128)(2,1)}), bf16[8192,288]{0,1:T(8,128)(2,1)}) %all-gather.3.cloned.1.call-update) | async-done | bytes 4718608 | tf_op jit(solution)/shard_map/all_gather | solution.py:101
  97.7 4.4 fusion.36
  103.7 9.6 %all-to-all-start.1 = ((bf16[128,32,256]{2,0,1:T(8,128)(2,1)}), bf16[128,32,256]{2,0,1:T(8,128)(2,1)S(1)}, u32[]{:S(2)}, u32[]{:S(2)}) async-start(bf16[128,32,256]{2,0,1:T(8,128)(2,1)} %bitcast.50), calls=%async_computation.1 | async-start | bytes 4194304 | tf_op jit(solution)/shard_map/all_to_all | solution.py:105
  113.3 3.2 copy.29
  116.5 88.0 %all-gather.5.cloned.1.call-done = f32[4096,288]{0,1:T(8,128)} async-done(((f32[128,288]{0,1:T(8,128)}), f32[4096,288]{0,1:T(8,128)}) %all-gather.5.cloned.1.call-update) | async-done | bytes 4718608 | tf_op jit(solution)/shard_map/all_gather | solution.py:108
  204.6 2.5 multiply_reduce_fusion.32
  207.1 9.5 %all-to-all-start.2 = ((bf16[128,32,256]{2,0,1:T(8,128)(2,1)}), bf16[128,32,256]{2,0,1:T(8,128)(2,1)}, u32[]{:S(2)}, u32[]{:S(2)}) async-start(bf16[128,32,256]{2,0,1:T(8,128)(2,1)} %bitcast.49), calls=%async_computation.2 | async-start | bytes 4194304 | tf_op jit(solution)/shard_map/all_to_all | solution.py:106
  216.7 8.7 %bitcast_multiply_fusion.2 = (f32[4096,256]{1,0:T(8,128)}, f32[4096,256]{1,0:T(8,128)}) fusion(bf16[128,32,256]{2,0,1:T(8,128)(2,1)S(1)} %all-to-all-done.1, f32[256]{0:T(256)S(1)} %copy-done.131, bf16[256,256]{1,0:T(8,128)(2,1)S(1)} %copy-done, f32[4096,288]{0,1:T(8,128)} %all-gather.5.cloned.1.call-done, f32[256]{0:T(256)S(1)} %copy-done.132, ...), kind=kOutput, calls=%fused_computation.23 | convolution fusion | flops 549453824 | bytes 14829568 | tf_op jit(solution)/shard_map/dot_general | solution.py:118
  225.4 5.0 reshape.167
  230.4 4.4 slice_add_fusion.22
  236.7 5.0 reshape.169
  241.7 4.0 fusion.30
  254.5 20.0 %multiply_reduce_fusion.1 = (f32[256,256]{1,0:T(8,128)}, f32[256,16,256]{2,1,0:T(8,128)S(1)}, f32[256,16,256]{2,1,0:T(8,128)S(1)}, f32[256,16,256]{2,1,0:T(8,128)}) fusion(f32[256,16]{1,0:T(8,128)S(1)} %get-tuple-element.99, f32[256,256]{1,0:T(8,128)} %get-tuple-element.77, f32[256,16]{1,0:T(8,128)} %get-tuple-element.117, ...), kind=kLoop, calls=%fused_computation.27 | loop fusion | flops 69140480 | bytes 21528576 | tf_op jit(solution)/shard_map/reduce_sum | solution.py:65
  274.5 6.4 multiply_reduce_fusion.3
  288.5 2.0 pad.53
  291.8 1.9 pad.52
  298.9 3.3 pad.55
  307.3 2.9 pad.57
  311.1 3.1 pad.56
  317.9 5.6 pad.58
  323.5 8.7 %pad.59 = f32[32,16,256]{2,1,0:T(8,128)} pad(f32[16,16,256]{2,1,0:T(8,128)} %add.351, f32[]{:T(128)} %constant.5.clone.1), padding=1_0_1x0_0_0x0_0_0 | pad | bytes 786436 | tf_op jit(solution)/shard_map/pad | solution.py:69
  332.2 2.1 add.353
  334.3 2.3 fusion.20
  336.7 11.6 %pad.61 = f32[64,16,256]{2,1,0:T(8,128)S(1)} pad(f32[32,16,256]{2,1,0:T(8,128)} %add.353, f32[]{:T(128)} %constant.5.clone.1), padding=1_0_1x0_0_0x0_0_0 | pad | bytes 1572868 | tf_op jit(solution)/shard_map/pad | solution.py:69
  350.1 15.6 %pad.60 = f32[64,16,256]{2,1,0:T(8,128)} pad(f32[32,16,256]{2,1,0:T(8,128)} %pad_maximum_fusion.3, f32[]{:T(128)} %constant.5.clone.1), padding=0_1_1x0_0_0x0_0_0 | pad | bytes 1572868 | tf_op jit(solution)/shard_map/pad | solution.py:69
  365.7 2.1 fusion.19
  370.1 23.1 %pad.62 = f32[128,16,256]{2,1,0:T(8,128)S(1)} pad(f32[64,16,256]{2,1,0:T(8,128)} %pad_maximum_fusion.2, f32[]{:T(128)} %constant.5.clone.1), padding=0_1_1x0_0_0x0_0_0 | pad | bytes 3145732 | tf_op jit(solution)/shard_map/pad | solution.py:69
  393.3 20.5 %pad.63 = f32[128,16,256]{2,1,0:T(8,128)} pad(f32[64,16,256]{2,1,0:T(8,128)S(1)} %copy-done.14, f32[]{:T(128)} %constant.5.clone.1), padding=1_0_1x0_0_0x0_0_0 | pad | bytes 3145732 | tf_op jit(solution)/shard_map/pad | solution.py:69
  413.7 3.5 add.357
  417.9 4.1 fusion.18
  422.8 9.2 %multiply_reduce_fusion.17 = f32[256,256]{1,0:T(8,128)} fusion(f32[256,16]{1,0:T(8,128)S(1)} %copy-done.103, f32[256,256]{1,0:T(8,128)S(1)} %copy-done.93, f32[256,16]{1,0:T(8,128)S(1)} %copy-done.128, f32[256,256]{1,0:T(8,128)S(1)} %copy-done.102, f32[16,256]{1,0:T(8,128)S(1)} %exponential_negate_fusion, f32[256,256]{1,0:T(8,128)S(1)} %copy-done.92, ...), kind=kLoop, calls=%fused_computation.43 | loop fusion | flops 35586048 | bytes 4620288 | tf_op jit(solution)/shard_map/reduce_sum | solution.py:65
  432.0 40.5 %pad.161 = f32[256,16,256]{2,1,0:T(8,128)} pad(f32[128,16,256]{2,1,0:T(8,128)S(1)} %copy-done.11, f32[]{:T(128)} %constant.5.clone.1), padding=1_0_1x0_0_0x0_0_0 | pad | bytes 6291460
  474.3 40.5 %pad.87 = f32[255,16,256]{2,1,0:T(8,128)} pad(f32[128,16,256]{2,1,0:T(8,128)S(1)} %pad_maximum_fusion.1, f32[]{:T(128)} %constant.5.clone.1), padding=0_0_1x0_0_0x0_0_0 | pad | bytes 6275076 | tf_op jit(solution)/shard_map/slice | solution.py:70
  514.9 8.7 %multiply_reduce_fusion.19 = f32[256,256]{1,0:T(8,128)S(1)} fusion(f32[256,16]{1,0:T(8,128)S(1)} %copy-done.105, f32[256,256]{1,0:T(8,128)} %get-tuple-element.86, f32[256,16]{1,0:T(8,128)} %get-tuple-element.126, f32[256,256]{1,0:T(8,128)} %get-tuple-element.87, f32[256,16]{1,0:T(8,128)} %get-tuple-element.127, f32[256,256]{1,0:T(8,128)} %get-tuple-element.65, ...), kind=kLoop, calls=%fused_computation.45 | loop fusion | flops 31391744 | bytes 4079616 | tf_op jit(solution)/shard_map/reduce_sum | solution.py:65
  523.8 6.3 multiply_reduce_fusion.21
  531.5 9.1 %multiply_reduce_fusion.29 = (f32[256,256]{1,0:T(8,128)S(1)}, f32[256,256]{1,0:T(8,128)S(1)}, f32[256,256]{1,0:T(8,128)S(1)}, f32[256,256]{1,0:T(8,128)S(1)}, f32[256,256]{1,0:T(8,128)S(1)}, /*index=5*/f32[256,256]{1,0:T(8,128)S(1)}) fusion(f32[256,16]{1,0:T(8,128)S(1)} %copy-done.113, f32[256,256]{1,0:T(8,128)S(1)} %copy-done.87, ...), kind=kLoop, calls=%fused_computation.55 | loop fusion | flops 27918336 | bytes 7716864 | tf_op jit(solution)/shard_map/reduce_sum | solution.py:65
  541.5 7.6 %multiply_reduce_fusion.23 = (f32[256,256]{1,0:T(8,128)S(1)}, f32[256,256]{1,0:T(8,128)S(1)}, f32[256,256]{1,0:T(8,128)S(1)}) fusion(f32[256,16]{1,0:T(8,128)S(1)} %copy-done.110, f32[256,256]{1,0:T(8,128)S(1)} %copy-done.81, f32[256,16]{1,0:T(8,128)S(1)} %copy-done.117, f32[256,256]{1,0:T(8,128)S(1)} %copy-done.84, f32[256,16]{1,0:T(8,128)S(1)} %copy-done.119, ...), kind=kLoop, calls=%fused_computation.49 | loop fusion | flops 27066368 | bytes 3555328 | tf_op jit(solution)/shard_map/reduce_sum | solution.py:65
  549.3 8.8 %multiply_reduce_fusion = (f32[256,256]{1,0:T(8,128)S(1)}, f32[256,256]{1,0:T(8,128)S(1)}, f32[256,256]{1,0:T(8,128)S(1)}, f32[256,256]{1,0:T(8,128)S(1)}, f32[256,256]{1,0:T(8,128)S(1)}, /*index=5*/f32[256,256]{1,0:T(8,128)S(1)}) fusion(f32[256,16]{1,0:T(8,128)S(1)} %copy-done.108, f32[16,256]{1,0:T(8,128)S(1)} %exponential_negate_fusion, ...), kind=kLoop, calls=%fused_computation.26 | loop fusion | flops 24772608 | bytes 7438336 | tf_op jit(solution)/shard_map/reduce_sum | solution.py:74
  562.1 8.8 %multiply_reduce_fusion.2 = (f32[256,256]{1,0:T(8,128)S(1)}, f32[256,256]{1,0:T(8,128)S(1)}, f32[256,256]{1,0:T(8,128)S(1)}, f32[256,256]{1,0:T(8,128)S(1)}, f32[256,256]{1,0:T(8,128)S(1)}, /*index=5*/f32[256,256]{1,0:T(8,128)S(1)}) fusion(f32[256,256]{1,0:T(8,128)S(1)} %copy-done.57, f32[256,16]{1,0:T(8,128)S(1)} %copy-done.50, ...), kind=kLoop, calls=%fused_computation.28 | loop fusion | flops 24772608 | bytes 7438336 | tf_op jit(solution)/shard_map/reduce_sum | solution.py:74
  572.5 7.2 %multiply_reduce_fusion.9 = (f32[256,256]{1,0:T(8,128)S(1)}, f32[256,256]{1,0:T(8,128)S(1)}, f32[256,256]{1,0:T(8,128)S(1)}, f32[256,256]{1,0:T(8,128)S(1)}) fusion(f32[256,16]{1,0:T(8,128)S(1)} %copy-done.46, f32[256,256]{1,0:T(8,128)S(1)} %copy-done.27, f32[256,16]{1,0:T(8,128)S(1)} %copy-done.40, f32[256,256]{1,0:T(8,128)S(1)} %copy-done.37, ...), kind=kLoop, calls=%fused_computation.35 | loop fusion | flops 20709376 | bytes 6946816 | tf_op jit(solution)/shard_map/reduce_sum | solution.py:65
  586.0 4.9 reshape.170
  590.9 3.3 fusion.14
  594.3 2.9 fusion.15
  597.1 52.1 %all_to_all.50 = bf16[32,128,256]{2,1,0:T(8,128)(2,1)S(1)} all-to-all(bf16[32,128,256]{2,1,0:T(8,128)(2,1)S(1)} %bitcast.48), channel_id=1, replica_groups=mesh['seq'=32,'batch'=8] {'seq'}, dimensions={0} | all-to-all | bytes 4194304 | tf_op jit(solution)/shard_map/all_to_all | solution.py:128
  (340 shorter events, 63.6 us)
Async XLA Ops:
  6.5 210.2 %copy-start = (bf16[256,256]{1,0:T(8,128)(2,1)S(1)}, bf16[256,256]{1,0:T(8,128)(2,1)}, u32[]{:S(2)}) copy-start(bf16[256,256]{1,0:T(8,128)(2,1)} %param.16) | copy-start | bytes 393220
  6.5 91.2 %all-gather.3.cloned.1.call-start = ((), (), s32[]{:S(2)}) async-start(), calls=%async_computation.4 | async-start | bytes 4866048 | tf_op jit(solution)/shard_map/all_gather | solution.py:101
  9.3 21.8 %all-to-all-start = ((bf16[32,5,256]{2,1,0:T(8,128)(2,1)}), bf16[32,5,256]{2,1,0:T(8,128)(2,1)S(1)}, u32[]{:S(2)}, u32[]{:S(2)}) async-start(bf16[32,5,256]{2,1,0:T(8,128)(2,1)} %broadcast_in_dim.7), calls=%async_computation | async-start | bytes 262144 | tf_op jit(solution)/shard_map/all_to_all | solution.py:15
  21.0 183.6 %all-gather.5.cloned.1.call-start = ((), (), s32[]{:S(2)}) async-start(), calls=%async_computation.5 | async-start | bytes 4866048 | tf_op jit(solution)/shard_map/all_gather | solution.py:108
  22.0 9.1 %collective-permute-start = (bf16[3,8192]{1,0:T(4,128)(2,1)S(1)}, bf16[3,8192]{1,0:T(4,128)(2,1)S(1)}, u32[]{:S(2)}, u32[]{:S(2)}) collective-permute-start(bf16[3,8192]{1,0:T(4,128)(2,1)S(1)} %slice.443), channel_id=1, source_target_pairs={{0,8},{8,16},{16,24},{24,32},{32,40},{40,48},{48,56},{56,64},{64,7... | collective-permute-start | bytes 147464 | tf_op jit(solution)/shard_map/ppermute | solution.py:10
  103.7 12.8 %copy-start.129 = (f32[16,256]{1,0:T(8,128)S(1)}, f32[16,256]{1,0:T(8,128)}, u32[]{:S(2)}) copy-start(f32[16,256]{1,0:T(8,128)} %param.18) | copy-start | bytes 49156
  103.7 103.4 %all-to-all-start.1 = ((bf16[128,32,256]{2,0,1:T(8,128)(2,1)}), bf16[128,32,256]{2,0,1:T(8,128)(2,1)S(1)}, u32[]{:S(2)}, u32[]{:S(2)}) async-start(bf16[128,32,256]{2,0,1:T(8,128)(2,1)} %bitcast.50), calls=%async_computation.1 | async-start | bytes 4194304 | tf_op jit(solution)/shard_map/all_to_all | solution.py:105
  116.5 100.2 %copy-start.131 = (f32[256]{0:T(256)S(1)}, f32[256]{0:T(256)}, u32[]{:S(2)}) copy-start(f32[256]{0:T(256)} %param.17) | copy-start | bytes 3076
  116.5 100.2 %copy-start.132 = (f32[256]{0:T(256)S(1)}, f32[256]{0:T(256)}, u32[]{:S(2)}) copy-start(f32[256]{0:T(256)} %param.15) | copy-start | bytes 3076
  207.1 18.3 %copy-start.12 = (bf16[128,32,256]{2,0,1:T(8,128)(2,1)}, bf16[128,32,256]{2,0,1:T(8,128)(2,1)S(1)}, u32[]{:S(2)}) copy-start(bf16[128,32,256]{2,0,1:T(8,128)(2,1)S(1)} %all-to-all-done.1) | copy-start | bytes 6291460
  207.1 387.1 %all-to-all-start.2 = ((bf16[128,32,256]{2,0,1:T(8,128)(2,1)}), bf16[128,32,256]{2,0,1:T(8,128)(2,1)}, u32[]{:S(2)}, u32[]{:S(2)}) async-start(bf16[128,32,256]{2,0,1:T(8,128)(2,1)} %bitcast.49), calls=%async_computation.2 | async-start | bytes 4194304 | tf_op jit(solution)/shard_map/all_to_all | solution.py:106
  234.9 39.7 %copy-start.19 = (f32[256,256]{1,0:T(8,128)}, f32[256,256]{1,0:T(8,128)S(1)}, u32[]{:S(2)}) copy-start(f32[256,256]{1,0:T(8,128)S(1)} %get-tuple-element.41) | copy-start | bytes 786436
  253.6 20.9 %copy-start.107 = (f32[256,16]{1,0:T(8,128)}, f32[256,16]{1,0:T(8,128)S(1)}, u32[]{:S(2)}) copy-start(f32[256,16]{1,0:T(8,128)S(1)} %get-tuple-element.99) | copy-start | bytes 49156
  253.6 20.9 %copy-start.49 = (f32[256,16]{1,0:T(8,128)}, f32[256,16]{1,0:T(8,128)S(1)}, u32[]{:S(2)}) copy-start(f32[256,16]{1,0:T(8,128)S(1)} %get-tuple-element.100) | copy-start | bytes 49156
  253.6 20.9 %copy-start.51 = (f32[256,16]{1,0:T(8,128)}, f32[256,16]{1,0:T(8,128)S(1)}, u32[]{:S(2)}) copy-start(f32[256,16]{1,0:T(8,128)S(1)} %get-tuple-element.101) | copy-start | bytes 49156
  253.6 20.9 %copy-start.53 = (f32[256,16]{1,0:T(8,128)}, f32[256,16]{1,0:T(8,128)S(1)}, u32[]{:S(2)}) copy-start(f32[256,16]{1,0:T(8,128)S(1)} %get-tuple-element.102) | copy-start | bytes 49156
  369.0 24.2 %copy-start.14 = (f32[64,16,256]{2,1,0:T(8,128)S(1)}, f32[64,16,256]{2,1,0:T(8,128)}, u32[]{:S(2)}) copy-start(f32[64,16,256]{2,1,0:T(8,128)} %add.355) | copy-start | bytes 3145732
  422.8 9.2 %copy-start.11 = (f32[128,16,256]{2,1,0:T(8,128)S(1)}, f32[128,16,256]{2,1,0:T(8,128)}, u32[]{:S(2)}) copy-start(f32[128,16,256]{2,1,0:T(8,128)} %add.357) | copy-start | bytes 6291460
  472.5 42.3 %copy-start.105 = (f32[256,16]{1,0:T(8,128)S(1)}, f32[256,16]{1,0:T(8,128)}, u32[]{:S(2)}) copy-start(f32[256,16]{1,0:T(8,128)} %get-tuple-element.107) | copy-start | bytes 49156
  531.5 9.9 %copy-start.110 = (f32[256,16]{1,0:T(8,128)S(1)}, f32[256,16]{1,0:T(8,128)}, u32[]{:S(2)}) copy-start(f32[256,16]{1,0:T(8,128)} %get-tuple-element.109) | copy-start | bytes 49156
  531.5 9.9 %copy-start.111 = (f32[256,16]{1,0:T(8,128)S(1)}, f32[256,16]{1,0:T(8,128)}, u32[]{:S(2)}) copy-start(f32[256,16]{1,0:T(8,128)} %get-tuple-element.110) | copy-start | bytes 49156
  531.5 9.9 %copy-start.112 = (f32[256,16]{1,0:T(8,128)S(1)}, f32[256,16]{1,0:T(8,128)}, u32[]{:S(2)}) copy-start(f32[256,16]{1,0:T(8,128)} %get-tuple-element.111) | copy-start | bytes 49156
  549.1 12.7 %copy-start.45 = (f32[256,16]{1,0:T(8,128)S(1)}, f32[256,16]{1,0:T(8,128)}, u32[]{:S(2)}) copy-start(f32[256,16]{1,0:T(8,128)} %get-tuple-element.98) | copy-start | bytes 49156
  549.1 12.7 %copy-start.47 = (f32[256,16]{1,0:T(8,128)S(1)}, f32[256,16]{1,0:T(8,128)}, u32[]{:S(2)}) copy-start(f32[256,16]{1,0:T(8,128)} %get-tuple-element.104) | copy-start | bytes 49156
  549.2 12.7 %copy-start.48 = (f32[256,16]{1,0:T(8,128)S(1)}, f32[256,16]{1,0:T(8,128)}, u32[]{:S(2)}) copy-start(f32[256,16]{1,0:T(8,128)} %get-tuple-element.105) | copy-start | bytes 49156
  549.2 12.7 %copy-start.50 = (f32[256,16]{1,0:T(8,128)S(1)}, f32[256,16]{1,0:T(8,128)}, u32[]{:S(2)}) copy-start(f32[256,16]{1,0:T(8,128)} %copy-done.49) | copy-start | bytes 49156
  549.2 12.7 %copy-start.57 = (f32[256,256]{1,0:T(8,128)S(1)}, f32[256,256]{1,0:T(8,128)}, u32[]{:S(2)}) copy-start(f32[256,256]{1,0:T(8,128)} %get-tuple-element.42) | copy-start | bytes 786436
  549.2 12.7 %copy-start.58 = (f32[256,256]{1,0:T(8,128)S(1)}, f32[256,256]{1,0:T(8,128)}, u32[]{:S(2)}) copy-start(f32[256,256]{1,0:T(8,128)} %get-tuple-element.46) | copy-start | bytes 786436
  549.2 12.7 %copy-start.59 = (f32[256,256]{1,0:T(8,128)S(1)}, f32[256,256]{1,0:T(8,128)}, u32[]{:S(2)}) copy-start(f32[256,256]{1,0:T(8,128)} %get-tuple-element.47) | copy-start | bytes 786436
  549.2 12.7 %copy-start.60 = (f32[256,256]{1,0:T(8,128)S(1)}, f32[256,256]{1,0:T(8,128)}, u32[]{:S(2)}) copy-start(f32[256,256]{1,0:T(8,128)} %get-tuple-element.48) | copy-start | bytes 786436
  549.2 12.7 %copy-start.61 = (f32[256,256]{1,0:T(8,128)S(1)}, f32[256,256]{1,0:T(8,128)}, u32[]{:S(2)}) copy-start(f32[256,256]{1,0:T(8,128)} %get-tuple-element.49) | copy-start | bytes 786436
  549.2 12.7 %copy-start.62 = (f32[256,256]{1,0:T(8,128)S(1)}, f32[256,256]{1,0:T(8,128)}, u32[]{:S(2)}) copy-start(f32[256,256]{1,0:T(8,128)} %get-tuple-element.50) | copy-start | bytes 786436
  549.2 12.7 %copy-start.104 = (f32[256,16]{1,0:T(8,128)S(1)}, f32[256,16]{1,0:T(8,128)}, u32[]{:S(2)}) copy-start(f32[256,16]{1,0:T(8,128)} %get-tuple-element.106) | copy-start | bytes 49156
  549.2 12.7 %copy-start.106 = (f32[256,16]{1,0:T(8,128)S(1)}, f32[256,16]{1,0:T(8,128)}, u32[]{:S(2)}) copy-start(f32[256,16]{1,0:T(8,128)} %get-tuple-element.107) | copy-start | bytes 49156
  562.0 9.6 %copy-start.94 = (f32[256,256]{1,0:T(8,128)S(1)}, f32[256,256]{1,0:T(8,128)}, u32[]{:S(2)}) copy-start(f32[256,256]{1,0:T(8,128)} %multiply_reduce_fusion.17) | copy-start | bytes 786436
  562.0 10.4 %copy-start.15 = (f32[256,16,256]{2,1,0:T(8,128)S(1)}, f32[256,16,256]{2,1,0:T(8,128)}, u32[]{:S(2)}) copy-start(f32[256,16,256]{2,1,0:T(8,128)} %get-tuple-element.40) | copy-start | bytes 12582916
  562.0 10.4 %copy-start.27 = (f32[256,256]{1,0:T(8,128)S(1)}, f32[256,256]{1,0:T(8,128)}, u32[]{:S(2)}) copy-start(f32[256,256]{1,0:T(8,128)} %get-tuple-element.81) | copy-start | bytes 786436
  562.0 10.4 %copy-start.29 = (f32[256,256]{1,0:T(8,128)S(1)}, f32[256,256]{1,0:T(8,128)}, u32[]{:S(2)}) copy-start(f32[256,256]{1,0:T(8,128)} %get-tuple-element.82) | copy-start | bytes 786436
  562.0 10.4 %copy-start.31 = (f32[256,256]{1,0:T(8,128)S(1)}, f32[256,256]{1,0:T(8,128)}, u32[]{:S(2)}) copy-start(f32[256,256]{1,0:T(8,128)} %get-tuple-element.83) | copy-start | bytes 786436
  562.0 10.4 %copy-start.33 = (f32[256,256]{1,0:T(8,128)S(1)}, f32[256,256]{1,0:T(8,128)}, u32[]{:S(2)}) copy-start(f32[256,256]{1,0:T(8,128)} %get-tuple-element.68) | copy-start | bytes 786436
  562.0 10.4 %copy-start.35 = (f32[256,256]{1,0:T(8,128)S(1)}, f32[256,256]{1,0:T(8,128)}, u32[]{:S(2)}) copy-start(f32[256,256]{1,0:T(8,128)} %get-tuple-element.69) | copy-start | bytes 786436
  562.0 10.4 %copy-start.37 = (f32[256,256]{1,0:T(8,128)S(1)}, f32[256,256]{1,0:T(8,128)}, u32[]{:S(2)}) copy-start(f32[256,256]{1,0:T(8,128)} %get-tuple-element.70) | copy-start | bytes 786436
  562.0 10.4 %copy-start.40 = (f32[256,16]{1,0:T(8,128)S(1)}, f32[256,16]{1,0:T(8,128)}, u32[]{:S(2)}) copy-start(f32[256,16]{1,0:T(8,128)} %copy-done.39) | copy-start | bytes 49156
  562.1 10.4 %copy-start.42 = (f32[256,16]{1,0:T(8,128)S(1)}, f32[256,16]{1,0:T(8,128)}, u32[]{:S(2)}) copy-start(f32[256,16]{1,0:T(8,128)} %get-tuple-element.122) | copy-start | bytes 49156
  562.1 10.4 %copy-start.44 = (f32[256,16]{1,0:T(8,128)S(1)}, f32[256,16]{1,0:T(8,128)}, u32[]{:S(2)}) copy-start(f32[256,16]{1,0:T(8,128)} %get-tuple-element.123) | copy-start | bytes 49156
  572.4 10.4 %copy-start.23 = (f32[256,256]{1,0:T(8,128)S(1)}, f32[256,256]{1,0:T(8,128)}, u32[]{:S(2)}) copy-start(f32[256,256]{1,0:T(8,128)} %get-tuple-element.22) | copy-start | bytes 786436
  572.4 11.2 %copy-start.22 = (f32[256,256]{1,0:T(8,128)S(1)}, f32[256,256]{1,0:T(8,128)}, u32[]{:S(2)}) copy-start(f32[256,256]{1,0:T(8,128)} %get-tuple-element.8) | copy-start | bytes 786436
  597.1 53.7 %copy-start.1 = (bf16[256,256]{1,0:T(8,128)(2,1)S(1)}, bf16[256,256]{1,0:T(8,128)(2,1)}, u32[]{:S(2)}) copy-start(bf16[256,256]{1,0:T(8,128)(2,1)} %param.16) | copy-start | bytes 393220
  (91 other events, 409.2 us)
Sparse Core Ops, SparseCore 0:
  9.8 87.9 all-gather.2
  102.3 102.2 all-gather.4
where the time goes:
time: 667 us; the launch traced here: 658 us
  local copies, waits for them, and re-layouts  226 us (34%)
  other arithmetic  167 us (25%)
  waiting for transfers between devices  149 us (22%)
  blocking collectives  52.1 us (8%)
  starting transfers between devices  34.2 us (5%)
  between operations  15.2 us (2%)
  matrix products  13.1 us (2%)
    pad x12, local copies, waits for them, and re-layouts, selective_scan(): _, through = lax.associative_scan(link_blocks, (totals, state), axis=0)  99.8 us
    all_gather x1, waiting for transfers between devices, local(): proj = lax.all_gather(local_proj, 'seq', axis=0, tiled=True)  88 us
    reduce_sum x8, other arithmetic, selective_scan(): local_parts.append(jnp.sum(c_now[:, :, None] * state, axis=1))  74.5 us
    all_gather x1, waiting for transfers between devices, local(): lax.all_gather(x_weight, 'seq', axis=0, tiled=True)  58.9 us
    all_to_all x1, blocking collectives, local(): return lax.all_to_all(gated, 'seq', split_axis=0, concat_axis=1, tiled=True)  52.1 us
    unnamed x267, local copies, waits for them, and re-layouts  46.1 us
    slice x1, local copies, waits for them, and re-layouts, selective_scan(): through[:blocks - 1]  40.5 us
    reduce_sum x2, other arithmetic, selective_scan(): jnp.sum(c_now[:, :, None] * jnp.exp(elapsed[place][:, None, :] * rate[Non...  17.5 us
  transfers between devices with their start and end apart: 6, of which 3 were waited for; matrix products, arithmetic and copies ran while one was open for 60% of the time, Pallas kernels for 0%

commit v1 on v0

v1 whole, which is shorter than its diff:
```python
import functools

import jax
import jax.numpy as jnp
from jax import lax
from jax.experimental import pallas as pl
from jax.experimental.pallas import tpu as pltpu
from jax.sharding import PartitionSpec as P

LOG2E = 1.4426950408889634
LANES = 128
F32 = jnp.float32
BF16 = jnp.bfloat16
VMEM_LIMIT = 48 * 1024 * 1024


def conv_proj_kernel(rows, width, states, x_ref, prior_ref, par_ref, xw_ref, xc_ref, proj_ref, bc_ref):
    shards, _, chans = par_ref.shape
    rank = proj_ref.shape[1]
    taps = states + 2
    halo = prior_ref.shape[0]

    @pl.when(pl.program_id(0) == 0)
    def _():
        proj_ref[...] = jnp.zeros_like(proj_ref)
        bc_ref[...] = jnp.zeros_like(bc_ref)

    for s in range(shards):
        at = slice(s * chans, (s + 1) * chans)
        full = jnp.concatenate([prior_ref[:, at].astype(F32), x_ref[:, at].astype(F32)], 0)
        total = jnp.broadcast_to(par_ref[s, taps + width : taps + width + 1, :], (rows, chans))
        for tap in range(width):
            start = halo - (width - 1) + tap
            total = total + par_ref[s, taps + tap : taps + tap + 1, :] * full[start : start + rows]
        xc = (total / (1.0 + jnp.exp(-total))).astype(BF16)
        xc_ref[:, at] = xc
        proj_ref[...] += jnp.dot(xc, xw_ref[s, :rank, :], preferred_element_type=F32)
        bc_ref[...] += lax.dot_general(
            xw_ref[s, rank:, :], xc, (((1,), (1,)), ((), ())), preferred_element_type=F32
        )


def spread(table_ref, turned):
    count, rows = turned.shape
    for t in range(rows):
        table_ref[t] = jnp.broadcast_to(turned[:, t : t + 1], (count, LANES))


def softplus(v):
    return jnp.maximum(v, 0.0) + jnp.log1p(jnp.exp(-jnp.abs(v)))


def step_kernel(states, proj_ref, bc_ref, gain_ref, dtw_ref, par_ref, xc_ref, step_ref, ends_ref,
                normed_ref, b_ref, drive_ref):
    shards, _, chans = dtw_ref.shape
    rows = proj_ref.shape[0]

    @pl.when(pl.program_id(0) == 0)
    def _():
        low = proj_ref[...]
        mean = jnp.mean(low * low, axis=1, keepdims=True)
        normed_ref[...] = (low * lax.rsqrt(mean + 1e-06) * gain_ref[...]).astype(BF16)
        spread(b_ref, bc_ref[:states])

    for s in range(shards):
        at = slice(s * chans, (s + 1) * chans)
        step = softplus(
            jnp.dot(normed_ref[...], dtw_ref[s], preferred_element_type=F32)
            + par_ref[s, states : states + 1, :]
        )
        step_ref[:, :, at] = step.reshape(rows // 8, 8, chans)
        drive = step * xc_ref[:, at].astype(F32)
        drive_ref[:, :, at] = drive.reshape(rows // 8, 8, chans)
        ends_ref[s, states : states + 8, :] = jnp.broadcast_to(
            jnp.sum(step, axis=0, keepdims=True), (8, chans)
        )
    pieces = [(s, l) for s in range(shards) for l in range(chans // LANES)]
    rates = [
        -LOG2E * jnp.exp(par_ref[s, :states, l * LANES : (l + 1) * LANES]) for s, l in pieces
    ]

    def advance(group, held):
        held = list(held)
        for r in range(8):
            b_now = b_ref[group * 8 + r]
            for i in range(len(pieces)):
                at = slice(i * LANES, (i + 1) * LANES)
                decay = jnp.exp2(step_ref[group, r : r + 1, at] * rates[i])
                held[i] = decay * held[i] + b_now * drive_ref[group, r : r + 1, at]
        return tuple(held)

    zero = jnp.zeros((states, LANES), F32)
    held = lax.fori_loop(0, rows // 8, advance, tuple(zero for _ in pieces))
    for i, (s, l) in enumerate(pieces):
        ends_ref[s, :states, l * LANES : (l + 1) * LANES] = held[i]


def gather_kernel(ny, nz, *refs):
    owns, outs = refs[:3], refs[3:6]
    send_sem, recv_sem, sib_sem = refs[6:]
    seq = lax.axis_index("seq")
    batch = lax.axis_index("batch")
    core = lax.rem(batch, 2)
    y, z = seq // nz, lax.rem(seq, nz)
    sibling = batch + 1 - 2 * core

    def place(yy, zz):
        return lax.rem(yy + ny, ny) * nz + lax.rem(zz + nz, nz)

    barrier = pltpu.get_barrier_semaphore()
    for there in (place(y + 1, z), place(y - 1, z), place(y, z + 1), place(y, z - 1)):
        pl.semaphore_signal(barrier, inc=1, device_id={"seq": there},
                            device_id_type=pl.DeviceIdType.MESH)
    pl.semaphore_signal(barrier, inc=1, device_id={"batch": sibling},
                        device_id_type=pl.DeviceIdType.MESH)
    pl.semaphore_wait(barrier, 5)

    def route(first, second, where, h):
        copies = []

        def source(part, fo, so):
            if fo == 0 and so == 0:
                size = owns[part].shape[0] // 2
                return owns[part].at[pl.ds(h * size, size)]
            return outs[part].at[where(fo, so), pl.ds(h * (outs[part].shape[1] // 2),
                                                      outs[part].shape[1] // 2)]

        def target(part, fo, so):
            size = outs[part].shape[1] // 2
            return outs[part].at[where(fo, so), pl.ds(h * size, size)]

        def push(part, fo, so, df, ds):
            copy = pltpu.make_async_remote_copy(
                src_ref=source(part, fo, so),
                dst_ref=target(part, fo, so),
                send_sem=send_sem.at[len(copies)],
                recv_sem=recv_sem.at[part, where(fo, so)],
                device_id={"seq": where(df, ds)},
                device_id_type=pl.DeviceIdType.MESH,
            )
            copy.start()
            copies.append(copy)

        def share(part, fo, so):
            copy = pltpu.make_async_remote_copy(
                src_ref=target(part, fo, so),
                dst_ref=target(part, fo, so),
                send_sem=send_sem.at[len(copies)],
                recv_sem=sib_sem.at[part, where(fo, so)],
                device_id={"batch": sibling},
                device_id_type=pl.DeviceIdType.MESH,
            )
            copy.start()
            copies.append(copy)

        def arrive(part, fo, so, sem):
            pltpu.make_async_remote_copy(
                src_ref=target(part, fo, so),
                dst_ref=target(part, fo, so),
                send_sem=send_sem.at[0],
                recv_sem=sem.at[part, where(fo, so)],
                device_id={"batch": sibling},
                device_id_type=pl.DeviceIdType.MESH,
            ).wait_recv()

        reach = {1: first // 2, -1: first - 1 - first // 2}

        def second_reach(fo, way):
            longer = second // 2 if fo % 2 == 0 else second - 1 - second // 2
            return longer if way == 1 else second - 1 - longer

        def launch_second(part, fo):
            for way in (1, -1):
                push(part, fo, 0, 0, way)

        def advance_second(part, fo, d):
            for way in (1, -1):
                if d <= second_reach(fo, way):
                    arrive(part, fo, -way * d, recv_sem)
                    if d < second_reach(fo, way):
                        push(part, fo, -way * d, 0, way)
                    share(part, fo, -way * d)

        for part in range(3):
            for way in (1, -1):
                push(part, 0, 0, way, 0)
            if part < 2:
                launch_second(part, 0)
        order = [0]
        for d in range(1, max(reach.values()) + 1):
            for part in range(3):
                for way in (1, -1):
                    if d <= reach[way]:
                        arrive(part, -way * d, 0, recv_sem)
                        if d < reach[way]:
                            push(part, -way * d, 0, way, 0)
                        if part < 2:
                            launch_second(part, -way * d)
                        share(part, -way * d, 0)
                        if part == 0:
                            order.append(-way * d)
        steps = max(second_reach(fo, way) for fo in order for way in (1, -1))
        for d in range(1, steps + 2):
            for fo in order:
                if d <= steps:
                    for part in range(2):
                        advance_second(part, fo, d)
                if d == 1:
                    launch_second(2, fo)
                else:
                    advance_second(2, fo, d - 1)
        for copy in copies:
            copy.wait_send()

    @pl.when(core == 0)
    def _():
        route(nz, ny, lambda fo, so: place(y + so, z + fo), 0)

    @pl.when(core == 1)
    def _():
        route(ny, nz, lambda fo, so: place(y + fo, z + so), 1)

    for part in range(3):
        outs[part][seq] = owns[part][...]

        def collect(k, carry):
            at = lax.rem(seq + k, ny * nz)
            size = outs[part].shape[1] // 2
            dst = outs[part].at[at, pl.ds(pl.multiple_of((1 - core) * size, size), size)]
            pltpu.make_async_remote_copy(
                src_ref=dst,
                dst_ref=dst,
                send_sem=send_sem.at[0],
                recv_sem=sib_sem.at[part, at],
                device_id={"batch": sibling},
                device_id_type=pl.DeviceIdType.MESH,
            ).wait_recv()
            return carry

        lax.fori_loop(1, ny * nz, collect, 0)


def exchange_kernel(states, ends_ref, alog_ref, starts_ref, held_ref, back_ref,
                    send_sem, recv_sem, send2_sem, recv2_sem):
    count, _, chans = ends_ref.shape
    me = lax.axis_index("seq")

    barrier = pltpu.get_barrier_semaphore()

    def greet(k, carry):
        pl.semaphore_signal(barrier, inc=1, device_id={"seq": lax.rem(me + k, count)},
                            device_id_type=pl.DeviceIdType.MESH)
        return carry

    lax.fori_loop(1, count, greet, 0)
    pl.semaphore_wait(barrier, count - 1)

    def out_copy(k):
        there = lax.rem(me + k, count)
        return pltpu.make_async_remote_copy(
            src_ref=ends_ref.at[there],
            dst_ref=held_ref.at[me],
            send_sem=send_sem.at[k],
            recv_sem=recv_sem.at[k],
            device_id={"seq": there},
            device_id_type=pl.DeviceIdType.MESH,
        )

    def back_copy(k):
        there = lax.rem(me + k, count)
        return pltpu.make_async_remote_copy(
            src_ref=back_ref.at[there],
            dst_ref=starts_ref.at[me],
            send_sem=send2_sem.at[k],
            recv_sem=recv2_sem.at[k],
            device_id={"seq": there},
            device_id_type=pl.DeviceIdType.MESH,
        )

    def in_wait(k, into, sem):
        source = lax.rem(me - k + count, count)
        pltpu.make_async_remote_copy(
            src_ref=into.at[source],
            dst_ref=into.at[source],
            send_sem=sem.at[k],
            recv_sem=sem.at[k],
            device_id={"seq": source},
            device_id_type=pl.DeviceIdType.MESH,
        ).wait_recv()

    def loop(step):
        def body(k, carry):
            step(k)
            return carry

        lax.fori_loop(1, count, body, 0)

    loop(lambda k: out_copy(k).start())
    held_ref[me] = ends_ref[me]
    rates = -LOG2E * jnp.exp(alog_ref[...])
    loop(lambda k: in_wait(k, held_ref, recv_sem))

    def link(i, held):
        back_ref[i] = held
        decay = jnp.exp2(held_ref[i, states : states + 1, :] * rates)
        return decay * held + held_ref[i, :states, :]

    lax.fori_loop(0, count, link, jnp.zeros((states, chans), F32))
    loop(lambda k: back_copy(k).start())
    starts_ref[me] = back_ref[me]
    loop(lambda k: out_copy(k).wait_send())
    loop(lambda k: in_wait(k, starts_ref, recv2_sem))
    loop(lambda k: back_copy(k).wait_send())


def scan_kernel(states, bc_ref, step_ref, xc_ref, gate_ref, par_ref, starts_ref, out_ref,
                b_ref, c_ref, drive_ref, part_ref):
    shards, _, chans = par_ref.shape
    rows = gate_ref.shape[0]

    @pl.when(pl.program_id(0) == 0)
    def _():
        spread(b_ref, bc_ref[:states])
        spread(c_ref, bc_ref[states:])

    drive_ref[...] = step_ref[...] * xc_ref[...].astype(F32).reshape(drive_ref.shape)
    pieces = [(s, l) for s in range(shards) for l in range(chans // LANES)]
    rates = [
        -LOG2E * jnp.exp(par_ref[s, :states, l * LANES : (l + 1) * LANES]) for s, l in pieces
    ]

    def advance(group, held):
        held = list(held)
        for r in range(8):
            t = group * 8 + r
            b_now = b_ref[t]
            c_now = c_ref[t]
            for i in range(len(pieces)):
                at = slice(i * LANES, (i + 1) * LANES)
                decay = jnp.exp2(step_ref[group, r : r + 1, at] * rates[i])
                held[i] = decay * held[i] + b_now * drive_ref[group, r : r + 1, at]
                seen = c_now * held[i]
                part_ref[i, pl.ds(pl.multiple_of(t * 8, 8), 8), :] = seen[:8] + seen[8:]
        return tuple(held)

    held = tuple(starts_ref[s, :, l * LANES : (l + 1) * LANES] for s, l in pieces)
    lax.fori_loop(0, rows // 8, advance, held)
    for i, (s, l) in enumerate(pieces):
        at = slice(i * LANES, (i + 1) * LANES)
        total = part_ref[i, pl.ds(0, rows, stride=8), :]
        for k in range(1, 8):
            total = total + part_ref[i, pl.ds(k, rows, stride=8), :]
        skip = par_ref[s, states + 1 : states + 2, l * LANES : (l + 1) * LANES]
        y_out = (total + skip * xc_ref[:, at].astype(F32)).astype(BF16).astype(F32)
        gate = gate_ref[:, at].astype(F32)
        out_ref[:, at] = (y_out * (gate / (1.0 + jnp.exp(-gate)))).astype(BF16)


def local(
    conv_input,
    gate_input,
    conv_weight,
    conv_bias,
    x_weight,
    dt_gain,
    dt_weight,
    dt_bias,
    a_log,
    skip,
):
    width = conv_weight.shape[0]
    rank = dt_weight.shape[0]
    states, chans = a_log.shape
    rows, inner = conv_input.shape
    count = lax.axis_size("seq")
    proj_cols = x_weight.shape[1]
    shards = 2
    block = shards * chans
    grid = inner // block
    params = pltpu.CompilerParams(
        dimension_semantics=("arbitrary",), vmem_limit_bytes=VMEM_LIMIT
    )

    prior = lax.ppermute(
        conv_input[rows - 8 :], "seq", [(i, i + 1) for i in range(count - 1)]
    )
    par_rows = 32
    par = jnp.concatenate(
        [
            a_log,
            dt_bias[None, :],
            skip[None, :],
            conv_weight.astype(F32),
            conv_bias.astype(F32)[None, :],
            jnp.zeros((par_rows - states - 2 - width - 1, chans), F32),
        ],
        0,
    )
    xw = jnp.concatenate([x_weight[:, :rank], x_weight[:, rank:].T], 0)
    xw_rows = xw.shape[0]
    ny, nz = 4, count // 4
    copies = 6 * (count - 1)
    vmem = pl.BlockSpec(memory_space=pltpu.VMEM)
    par, xw, dtw = pl.pallas_call(
        functools.partial(gather_kernel, ny, nz),
        in_specs=[vmem] * 3,
        out_specs=[vmem] * 3,
        out_shape=[
            jax.ShapeDtypeStruct((count, par_rows, chans), F32),
            jax.ShapeDtypeStruct((count, xw_rows, chans), BF16),
            jax.ShapeDtypeStruct((count, rank, chans), BF16),
        ],
        scratch_shapes=[
            pltpu.SemaphoreType.DMA((copies,)),
            pltpu.SemaphoreType.DMA((3, count)),
            pltpu.SemaphoreType.DMA((3, count)),
        ],
        compiler_params=pltpu.CompilerParams(
            collective_id=0, has_side_effects=True, vmem_limit_bytes=VMEM_LIMIT
        ),
        name="gather",
    )(par, xw, dt_weight)

    whole = lambda *shape: pl.BlockSpec(shape, lambda i: (0,) * len(shape))
    columns = lambda height: pl.BlockSpec((height, block), lambda i: (0, i))
    stacked = lambda *shape: pl.BlockSpec((shards, *shape), lambda i: (i, 0, 0))
    tiled = pl.BlockSpec((rows // 8, 8, block), lambda i: (0, 0, i))

    xc, proj, bc = pl.pallas_call(
        functools.partial(conv_proj_kernel, rows, width, states),
        grid=(grid,),
        in_specs=[columns(rows), columns(8), stacked(par_rows, chans), stacked(xw_rows, chans)],
        out_specs=[columns(rows), whole(rows, rank), whole(2 * states, rows)],
        out_shape=[
            jax.ShapeDtypeStruct((rows, inner), BF16),
            jax.ShapeDtypeStruct((rows, rank), F32),
            jax.ShapeDtypeStruct((2 * states, rows), F32),
        ],
        compiler_params=params,
        cost_estimate=pl.CostEstimate(
            flops=700_000_000, bytes_accessed=9_000_000, transcendentals=2_000_000
        ),
        name="conv_proj",
    )(conv_input, prior, par, xw)

    step, ends = pl.pallas_call(
        functools.partial(step_kernel, states),
        grid=(grid,),
        in_specs=[
            whole(rows, rank),
            whole(2 * states, rows),
            whole(1, rank),
            stacked(rank, chans),
            stacked(par_rows, chans),
            columns(rows),
        ],
        out_specs=[tiled, stacked(states + 8, chans)],
        out_shape=[
            jax.ShapeDtypeStruct((rows // 8, 8, inner), F32),
            jax.ShapeDtypeStruct((count, states + 8, chans), F32),
        ],
        scratch_shapes=[
            pltpu.VMEM((rows, rank), BF16),
            pltpu.VMEM((rows, states, LANES), F32),
            pltpu.VMEM((rows // 8, 8, block), F32),
        ],
        compiler_params=params,
        cost_estimate=pl.CostEstimate(
            flops=700_000_000, bytes_accessed=11_000_000, transcendentals=18_000_000
        ),
        name="step_ends",
    )(proj, bc, dt_gain[None, :], dtw, par, xc)

    starts = pl.pallas_call(
        functools.partial(exchange_kernel, states),
        in_specs=[vmem] * 2,
        out_specs=vmem,
        out_shape=jax.ShapeDtypeStruct((count, states, chans), F32),
        scratch_shapes=[
            pltpu.VMEM((count, states + 8, chans), F32),
            pltpu.VMEM((count, states, chans), F32),
            *[pltpu.SemaphoreType.DMA((count,)) for _ in range(4)],
        ],
        compiler_params=pltpu.CompilerParams(
            collective_id=1, has_side_effects=True, vmem_limit_bytes=VMEM_LIMIT
        ),
        name="exchange",
    )(ends, a_log)

    return pl.pallas_call(
        functools.partial(scan_kernel, states),
        grid=(grid,),
        in_specs=[
            whole(2 * states, rows),
            tiled,
            columns(rows),
            columns(rows),
            stacked(par_rows, chans),
            stacked(states, chans),
        ],
        out_specs=columns(rows),
        out_shape=jax.ShapeDtypeStruct((rows, inner), BF16),
        scratch_shapes=[
            pltpu.VMEM((rows, states, LANES), F32),
            pltpu.VMEM((rows, states, LANES), F32),
            pltpu.VMEM((rows // 8, 8, block), F32),
            pltpu.VMEM((block // LANES, rows * 8, LANES), F32),
        ],
        compiler_params=params,
        cost_estimate=pl.CostEstimate(
            flops=100_000_000, bytes_accessed=11_000_000, transcendentals=18_000_000
        ),
        name="scan_gate",
    )(bc, step, xc, gate_input, par, starts)


def solution(mesh):
    return jax.shard_map(
        local,
        mesh=mesh,
        in_specs=(
            P(("batch", "seq"), None),
            P(("batch", "seq"), None),
            P(None, "seq"),
            P("seq"),
            P("seq", None),
            P(),
            P(None, "seq"),
            P("seq"),
            P(None, "seq"),
            P("seq"),
        ),
        out_specs=P(("batch", "seq"), None),
        check_vma=False,
    )
```

time: 667 us -> 161 us (0.24); the launches traced: 658 us -> 160 us
  local copies, waits for them, and re-layouts: 226 us -> 8.75 us
  other arithmetic: 167 us -> 0.67 us
  waiting for transfers between devices: 149 us -> 0.01 us
  Pallas kernels: 0 us -> 147 us
  blocking collectives: 52.1 us -> 0 us
  starting transfers between devices: 34.2 us -> 3.83 us
  between operations: 15.2 us -> 0.12 us
  matrix products: 13.1 us -> 0 us
    all_gather x2 -> x0, waiting for transfers between devices: 147 us -> none  [the longest x1 88 us: local(): proj = lax.all_gather(local_proj, 'seq', axis=0, tiled=True)]
    pallas_call x0 -> x5, Pallas kernels: none -> 147 us  [the longest x1 48.2 us: local(): pl.pallas_call(functools.partial(gather_kernel, ny, nz), in_specs=[vmem]...]
    pad x12 -> x0, local copies, waits for them, and re-layouts: 99.8 us -> none  [selective_scan(): _, through = lax.associative_scan(link_blocks, (totals, state), axis=0)]
    reduce_sum x11 -> x0, other arithmetic: 94.6 us -> none  [the longest x8 74.5 us: selective_scan(): local_parts.append(jnp.sum(c_now[:, :, None] * state, axis=1))]
    slice x15 -> x2, local copies, waits for them, and re-layouts: 56.2 us -> 1.83 us  [the longest x1 0.91 us: local(): xw = jnp.concatenate([x_weight[:, :rank], x_weight[:, rank:].T], 0)]
    all_to_all x1 -> x0, blocking collectives: 52.1 us -> none  [local(): return lax.all_to_all(gated, 'seq', split_axis=0, concat_axis=1, tiled=True)]
    unnamed x267 -> x13, local copies, waits for them, and re-layouts: 46.1 us -> 4.64 us
    all_to_all x3 -> x0, starting transfers between devices: 30.8 us -> none  [the longest x1 11.7 us: from_everyone(): return lax.all_to_all(copies, axis, split_axis=0, concat_axis=0, tiled=True)]
  transfers between devices with their start and end apart: 6 -> 1, of which waited for: 3 -> 0; matrix products, arithmetic and copies ran while one was open for 60% -> 2% of each run, Pallas kernels for 0% -> 30%
where the time goes in v1:
time: 161 us; the launch traced here: 160 us
  Pallas kernels  147 us (91%)
  local copies, waits for them, and re-layouts  8.75 us (5%)
  starting transfers between devices  3.83 us (2%)
    pallas_call x1, Pallas kernels, local(): pl.pallas_call(functools.partial(gather_kernel, ny, nz), in_specs=[vmem]...  48.2 us
    pallas_call x1, Pallas kernels, local(): pl.pallas_call(functools.partial(exchange_kernel, states), in_specs=[vmem...  38.2 us
    pallas_call x1, Pallas kernels, local(): pl.pallas_call(functools.partial(scan_kernel, states), grid=(grid,), in_s...  27.3 us
    pallas_call x1, Pallas kernels, local(): pl.pallas_call(functools.partial(step_kernel, states), grid=(grid,), in_s...  21.2 us
    pallas_call x1, Pallas kernels, local(): pl.pallas_call(functools.partial(conv_proj_kernel, rows, width, states),...  11.7 us
    unnamed x13, local copies, waits for them, and re-layouts  4.64 us
    ppermute x1, starting transfers between devices, local(): lax.ppermute(conv_input[rows - 8:], 'seq', [(i, i + 1) for i in range(cou...  3.83 us
  transfers between devices with their start and end apart: 1, of which 0 were waited for; matrix products, arithmetic and copies ran while one was open for 2% of the time, Pallas kernels for 30%

profile of v1, /device:TPU:8, one launch (start us, length us, event | category | flops | bytes accessed | tf_op | source)
XLA Modules:
  0.0 160.0 jit_solution(1408489077360603487)
XLA Ops:
  0.0 0.9 slice.9
  0.9 3.8 %collective-permute-start = (bf16[8,8192]{1,0:T(8,128)(2,1)S(1)}, bf16[8,8192]{1,0:T(8,128)(2,1)S(1)}, u32[]{:S(2)}, u32[]{:S(2)}) collective-permute-start(bf16[8,8192]{1,0:T(8,128)(2,1)S(1)} %slice.9), channel_id=1, source_target_pairs={{0,8},{8,16},{16,24},{24,32},{32,40},{40,48},{48,56},{56,64},{64,7... | collective-permute-start | bytes 393224 | tf_op jit(solution)/shard_map/ppermute | solution.py:384
  4.8 0.7 slice_bitcast_fusion
  5.5 0.9 slice.10
  6.4 0.7 broadcast_in_dim.24
  7.0 0.1 copy.12
  7.2 1.6 concatenate.6.refs_0_
  8.8 0.0 copy-start.1
  8.8 0.9 copy-done.1
  9.7 48.2 %gather.1 = (f32[32,32,256]{2,1,0:T(8,128)S(1)}, bf16[32,288,256]{2,1,0:T(8,128)(2,1)}, bf16[32,256,256]{2,1,0:T(8,128)(2,1)S(1)}) custom-call(f32[32,256]{1,0:T(8,128)S(1)} %concatenate.6.refs_0_, bf16[288,256]{1,0:T(8,128)(2,1)S(1)} %pad_maximum_fusion.refs_1_, bf16[256,256]{1,0:T(8,128)(2,1)S(1)} %copy-done.1), custom_call_target="tpu_custom_call" | custom-call | tf_op jit(solution)/shard_map/gather/pallas_call | solution.py:404
  57.9 0.0 copy-start.3
  57.9 2.0 %copy-done.3 = bf16[32,256,256]{2,1,0:T(8,128)(2,1)} copy-done((bf16[32,256,256]{2,1,0:T(8,128)(2,1)}, bf16[32,256,256]{2,1,0:T(8,128)(2,1)S(1)}, u32[]{:S(2)}) %copy-start.3) | copy-done | bytes 4194328
  59.9 0.0 collective-permute-done.prior_ref
  59.9 0.0 copy-start
  59.9 1.6 copy-done
  61.5 0.0 copy-start.5
  61.5 11.7 %conv_proj.1 = (bf16[128,8192]{1,0:T(8,128)(2,1)S(1)}, f32[128,256]{1,0:T(8,128)S(1)}, f32[32,128]{1,0:T(8,128)S(1)}) custom-call(bf16[128,8192]{1,0:T(8,128)(2,1)S(1)} %copy-done, bf16[8,8192]{1,0:T(8,128)(2,1)S(1)} %collective-permute-done.prior_ref, f32[32,32,256]{2,1,0:T(8,128)S(1)} %get-tuple-element.13.par_ref, ...), custom_call_target="tpu_custom_call" | custom-call | flops 700000000 | bytes 9000000 | tf_op jit(solution)/shard_map/conv_proj/pallas_call | solution.py:429
  73.2 0.0 copy-done.5
  73.2 0.0 copy-start.2
  73.2 0.0 copy-start.4
  73.2 21.2 %step_ends.1 = (f32[16,8,8192]{2,1,0:T(8,128)}, f32[32,24,256]{2,1,0:T(8,128)S(1)}) custom-call(f32[128,256]{1,0:T(8,128)S(1)} %get-tuple-element.16.proj_ref, f32[32,128]{1,0:T(8,128)S(1)} %get-tuple-element.15.bc_ref, f32[1,256]{1,0:T(1,128)S(1)} %bitcast.6, bf16[32,256,256]{2,1,0:T(8,128)(2,1)} %copy-done.3, ...), custom_call_target="tpu_custom_call" | custom-call | flops 700000000 | bytes 11000000 | tf_op jit(solution)/shard_map/step_ends/pallas_call | solution.py:446
  94.4 0.0 copy-done.2
  94.4 38.2 %exchange.1.starts_ref = f32[32,16,256]{2,1,0:T(8,128)S(1)} custom-call(f32[32,24,256]{2,1,0:T(8,128)S(1)} %get-tuple-element.20.ends_ref, f32[16,256]{1,0:T(8,128)S(1)} %copy-done.2), custom_call_target="tpu_custom_call" | custom-call | tf_op jit(solution)/shard_map/exchange/pallas_call | solution.py:474
  132.7 0.0 copy-done.4
  132.7 27.3 %scan_gate.1 = bf16[128,8192]{1,0:T(8,128)(2,1)} custom-call(f32[32,128]{1,0:T(8,128)S(1)} %get-tuple-element.15.bc_ref, f32[16,8,8192]{2,1,0:T(8,128)} %get-tuple-element.19.step_ref, bf16[128,8192]{1,0:T(8,128)(2,1)S(1)} %get-tuple-element.18.xc_ref, bf16[128,8192]{1,0:T(8,128)(2,1)S(1)} %copy-done.4, f32[32,32,256]{2,1,0:T(8,128)S(1)} %get-tuple-element.13.par_ref, ...), custom_call_target="tpu_custom_call" | custom-call | flops 100000000 | bytes 11000000 | tf_op jit(solution)/shard_map/scan_gate/pallas_call | solution.py:490
  (2 shorter events, 0.0 us)
Async XLA Ops:
  0.9 59.0 %collective-permute-start = (bf16[8,8192]{1,0:T(8,128)(2,1)S(1)}, bf16[8,8192]{1,0:T(8,128)(2,1)S(1)}, u32[]{:S(2)}, u32[]{:S(2)}) collective-permute-start(bf16[8,8192]{1,0:T(8,128)(2,1)S(1)} %slice.9), channel_id=1, source_target_pairs={{0,8},{8,16},{16,24},{24,32},{32,40},{40,48},{48,56},{56,64},{64,7... | collective-permute-start | bytes 393224 | tf_op jit(solution)/shard_map/ppermute | solution.py:384
  8.8 0.9 copy-start.1
  57.9 2.0 %copy-start.3 = (bf16[32,256,256]{2,1,0:T(8,128)(2,1)}, bf16[32,256,256]{2,1,0:T(8,128)(2,1)S(1)}, u32[]{:S(2)}) copy-start(bf16[32,256,256]{2,1,0:T(8,128)(2,1)S(1)} %get-tuple-element.17.dtw_ref) | copy-start | bytes 12582916
  59.9 1.6 copy-start
  61.5 11.7 %copy-start.5 = (f32[256]{0:T(256)S(1)}, f32[256]{0:T(256)}, u32[]{:S(2)}) copy-start(f32[256]{0:T(256)} %param.15) | copy-start | bytes 3076
  73.2 21.2 %copy-start.2 = (f32[16,256]{1,0:T(8,128)S(1)}, f32[16,256]{1,0:T(8,128)}, u32[]{:S(2)}) copy-start(f32[16,256]{1,0:T(8,128)} %alog_ref.1) | copy-start | bytes 49156
  73.2 59.4 %copy-start.4 = (bf16[128,8192]{1,0:T(8,128)(2,1)S(1)}, bf16[128,8192]{1,0:T(8,128)(2,1)}, u32[]{:S(2)}) copy-start(bf16[128,8192]{1,0:T(8,128)(2,1)} %gate_ref.1) | copy-start | bytes 6291460

commit v2 on v0

v2 whole, which is shorter than its diff:
```python
import functools

import jax
import jax.numpy as jnp
from jax import lax
from jax.experimental import pallas as pl
from jax.experimental.pallas import tpu as pltpu
from jax.sharding import PartitionSpec as P

LOG2E = 1.4426950408889634
LANES = 128
F32 = jnp.float32
BF16 = jnp.bfloat16
VMEM_LIMIT = 60 * 1024 * 1024
PAR, XW, DTW = 0, 1, 2


def silu(v):
    return v / (1.0 + jnp.exp(-v))


def softplus(v):
    return jnp.maximum(v, 0.0) + jnp.log1p(jnp.exp(-jnp.abs(v)))


def spread(table_ref, turned):
    count, rows = turned.shape
    for t in range(rows):
        table_ref[t] = jnp.broadcast_to(turned[:, t : t + 1], (count, LANES))


def zigzag(j):
    return -(j + 1) // 2 if j % 2 else j // 2


class Route:
    def __init__(self, first, second, where, h, owns, outs, send_sem, recv_sem, sib_sem, sibling):
        self.first, self.second, self.where, self.h = first, second, where, h
        self.owns, self.outs = owns, outs
        self.send_sem, self.recv_sem, self.sib_sem = send_sem, recv_sem, sib_sem
        self.sibling = sibling
        self.sent = []
        self.reach = {1: first // 2, -1: first - 1 - first // 2}

    def target(self, part, fo, so):
        size = self.outs[part].shape[1] // 2
        return self.outs[part].at[self.where(fo, so), pl.ds(self.h * size, size)]

    def source(self, part, fo, so):
        if fo == 0 and so == 0:
            size = self.owns[part].shape[0] // 2
            return self.owns[part].at[pl.ds(self.h * size, size)]
        return self.target(part, fo, so)

    def send(self, part, fo, so, sem, device):
        pltpu.make_async_remote_copy(
            src_ref=self.source(part, fo, so),
            dst_ref=self.target(part, fo, so),
            send_sem=self.send_sem.at[len(self.sent)],
            recv_sem=sem.at[part, self.where(fo, so)],
            device_id=device,
            device_id_type=pl.DeviceIdType.MESH,
        ).start()
        self.sent.append(part)

    def push(self, part, fo, so, df, ds):
        self.send(part, fo, so, self.recv_sem, {"seq": self.where(df, ds)})

    def share(self, part, fo, so):
        self.send(part, fo, so, self.sib_sem, {"batch": self.sibling})

    def arrive(self, part, fo, so):
        pltpu.make_async_remote_copy(
            src_ref=self.target(part, fo, so),
            dst_ref=self.target(part, fo, so),
            send_sem=self.send_sem.at[0],
            recv_sem=self.recv_sem.at[part, self.where(fo, so)],
            device_id={"batch": self.sibling},
            device_id_type=pl.DeviceIdType.MESH,
        ).wait_recv()

    def drain(self):
        for i, part in enumerate(self.sent):
            pltpu.make_async_remote_copy(
                src_ref=self.target(part, 0, 0),
                dst_ref=self.target(part, 0, 0),
                send_sem=self.send_sem.at[i],
                recv_sem=self.recv_sem.at[part, self.where(0, 0)],
                device_id={"batch": self.sibling},
                device_id_type=pl.DeviceIdType.MESH,
            ).wait_send()

    def second_reach(self, fo, way):
        longer = self.second // 2 if fo % 2 == 0 else self.second - 1 - self.second // 2
        return longer if way == 1 else self.second - 1 - longer

    def launch_second(self, part, fo):
        for way in (1, -1):
            self.push(part, fo, 0, 0, way)

    def open(self):
        for part in (PAR, XW, DTW):
            for way in (1, -1):
                self.push(part, 0, 0, way, 0)
            if part != DTW:
                self.launch_second(part, 0)

    def first_step(self, d):
        for part in (PAR, XW, DTW):
            for way in (1, -1):
                if d <= self.reach[way]:
                    self.arrive(part, -way * d, 0)
                    if d < self.reach[way]:
                        self.push(part, -way * d, 0, way, 0)
                    if part != DTW:
                        self.launch_second(part, -way * d)
                    self.share(part, -way * d, 0)

    def second_step(self, part, fo, d, way):
        if d <= self.second_reach(fo, way):
            self.arrive(part, fo, -way * d)
            if d < self.second_reach(fo, way):
                self.push(part, fo, -way * d, 0, way)
            self.share(part, fo, -way * d)


class ZFirst(Route):
    def piece(self, parts, m):
        order = [zigzag(j) for j in range(self.first)]
        if m < self.first:
            for part in parts:
                for way in (1, -1):
                    self.second_step(part, order[m], 1, way)
        if 1 <= m:
            for d in range(2, self.second // 2 + 1):
                for part in parts:
                    for way in (1, -1):
                        self.second_step(part, order[m - 1], d, way)

    def launch(self, m):
        self.launch_second(DTW, zigzag(m))


class YFirst(Route):
    def piece(self, parts, m):
        if 1 <= m < self.second:
            so = zigzag(m)
            for part in parts:
                for j in range(self.first):
                    fo = zigzag(j)
                    way = -1 if so > 0 else 1
                    d = abs(so)
                    if d <= self.second_reach(fo, way):
                        self.second_step(part, fo, d, way)
                    elif so == -(self.second // 2):
                        self.second_step(part, fo, d, -way)

    def launch(self, m):
        if m < self.first:
            self.launch_second(DTW, zigzag(m))


def mixer_kernel(ny, nz, x_hbm, gate_hbm, cw_ref, cb_ref, xw_ref, gain_ref, dtw_ref, dtb_ref,
                 alog_ref, skip_ref, halo_ref, out_hbm,
                 x_ref, gate_ref, out_ref, prior_ref, parown_ref, xwown_ref, par_ref, xwall_ref,
                 dtwall_ref, xc_ref, proj_ref, bc_ref, normed_ref, b_ref, c_ref, step_ref,
                 drive_ref, part_ref, ends_ref, sums_ref, heldends_ref, heldsums_ref, back_ref,
                 starts_ref,
                 load_sem, store_sem, halo_sem, send_sem, recv_sem, sib_sem, ends_sem, sums_sem,
                 back_sem):
    count = ny * nz
    rows, inner = x_ref.shape
    width = cw_ref.shape[0]
    states, chans = alog_ref.shape
    rank = proj_ref.shape[1]
    taps = states + 2
    seq = lax.axis_index("seq")
    batch = lax.axis_index("batch")
    core = lax.rem(batch, 2)
    y, z = seq // nz, lax.rem(seq, nz)
    sibling = batch + 1 - 2 * core
    mesh_id = pl.DeviceIdType.MESH

    def place(yy, zz):
        return lax.rem(yy + ny, ny) * nz + lax.rem(zz + nz, nz)

    load_x = pltpu.make_async_copy(x_hbm, x_ref, load_sem.at[0])
    load_gate = pltpu.make_async_copy(gate_hbm, gate_ref, load_sem.at[1])
    load_x.start()
    load_gate.start()

    barrier = pltpu.get_barrier_semaphore()
    after, before = lax.rem(seq + 1, count), lax.rem(seq + count - 1, count)
    for there in (place(y + 1, z), place(y - 1, z), place(y, z + 1), place(y, z - 1), after,
                  before):
        pl.semaphore_signal(barrier, inc=1, device_id={"seq": there}, device_id_type=mesh_id)
    pl.semaphore_signal(barrier, inc=1, device_id={"batch": sibling}, device_id_type=mesh_id)

    parown_ref[...] = jnp.zeros_like(parown_ref)
    parown_ref[:states] = alog_ref[...]
    parown_ref[states : states + 1] = dtb_ref[...]
    parown_ref[states + 1 : states + 2] = skip_ref[...]
    parown_ref[taps : taps + width] = cw_ref[...].astype(F32)
    parown_ref[taps + width : taps + width + 1] = cb_ref[...].astype(F32)
    xwown_ref[:rank] = xw_ref[:, :rank]
    tail = xw_ref[:, rank:].astype(F32)
    tail = jnp.concatenate([tail, jnp.zeros((chans, LANES - tail.shape[1]), F32)], 1)
    xwown_ref[rank:] = tail.T[: 2 * states].astype(BF16)
    owns, outs = (parown_ref, xwown_ref, dtw_ref), (par_ref, xwall_ref, dtwall_ref)
    proj_ref[...] = jnp.zeros_like(proj_ref)
    bc_ref[...] = jnp.zeros_like(bc_ref)
    for part in (PAR, XW, DTW):
        outs[part][seq] = owns[part][...]

    pl.semaphore_wait(barrier, 7)
    shared = (owns, outs, send_sem, recv_sem, sib_sem, sibling)
    routes = (
        ZFirst(nz, ny, lambda fo, so: place(y + so, z + fo), 0, *shared),
        YFirst(ny, nz, lambda fo, so: place(y + fo, z + so), 1, *shared),
    )

    def both(act):
        for h in range(2):
            @pl.when(core == h)
            def _():
                act(routes[h])

    halo = pltpu.make_async_remote_copy(
        src_ref=halo_ref, dst_ref=prior_ref, send_sem=halo_sem.at[0], recv_sem=halo_sem.at[1],
        device_id={"seq": after}, device_id_type=mesh_id,
    )
    both(lambda r: r.open())
    halo.start()

    def silu_gate(i, carry):
        at = pl.ds(pl.multiple_of(i * chans, chans), chans)
        gate_ref[:, at] = silu(gate_ref[:, at].astype(F32)).astype(BF16)
        return carry

    def fill(d):
        pass

    load_x.wait()
    load_gate.wait()
    longest = max(r.reach[1] for r in routes)
    for d in range(1, longest + 1):
        both(lambda r: r.first_step(d))
        fill(d)
    halo.wait_recv()

    def sibling_wait(part, at):
        size = outs[part].shape[1] // 2
        dst = outs[part].at[at, pl.ds(pl.multiple_of((1 - core) * size, size), size)]
        pltpu.make_async_remote_copy(
            src_ref=dst, dst_ref=dst, send_sem=send_sem.at[0], recv_sem=sib_sem.at[part, at],
            device_id={"batch": sibling}, device_id_type=mesh_id,
        ).wait_recv()

    first_rows = jnp.where(seq > 0, 1.0, 0.0)

    def conv_shard(s):
        at = pl.ds(pl.multiple_of(s * chans, chans), chans)
        prior = prior_ref[:, at].astype(F32) * first_rows
        full = jnp.concatenate([jnp.zeros_like(prior), prior, x_ref[:, at].astype(F32)], 0)
        lead = 2 * prior.shape[0] - (width - 1)
        total = jnp.broadcast_to(par_ref[s, taps + width : taps + width + 1, :], (rows, chans))
        for tap in range(width):
            total = total + par_ref[s, taps + tap : taps + tap + 1, :] * full[
                lead + tap : lead + tap + rows
            ]
        xc = silu(total).astype(BF16)
        xc_ref[s] = xc
        proj_ref[...] += jnp.dot(xc, xwall_ref[s, :rank, :], preferred_element_type=F32)
        bc_ref[...] += lax.dot_general(
            xwall_ref[s, rank:, :], xc, (((1,), (1,)), ((), ())), preferred_element_type=F32
        )

    def pair(m, p):
        dz = jnp.where(lax.rem(m, 2) == 1, -((m + 1) // 2), m // 2)
        return place(y + p, z + dz), place(y - p - 1 + ny, z + dz)

    def conv_group(m):
        def body(p, carry):
            sa, sb = pair(m, p)
            for j, s in enumerate((sa, sb)):
                if j == 0 and m == 0:
                    @pl.when(p > 0)
                    def _():
                        sibling_wait(PAR, s)
                        sibling_wait(XW, s)
                else:
                    sibling_wait(PAR, s)
                    sibling_wait(XW, s)
            conv_shard(sa)
            conv_shard(sb)
            return carry

        lax.fori_loop(0, ny // 2, body, 0)

    for m in range(nz + 1):
        def act(r):
            r.piece((PAR, XW), m)
            if m < nz:
                r.launch(m)
        both(act)
        if m > 0:
            conv_group(m - 1)

    low = proj_ref[...]
    mean = jnp.mean(low * low, axis=1, keepdims=True)
    normed_ref[...] = (low * lax.rsqrt(mean + 1e-06) * gain_ref[...]).astype(BF16)
    spread(b_ref, bc_ref[:states])

    blocks = chans // LANES

    def rates_of(s):
        return [
            -LOG2E * jnp.exp(par_ref[s, :states, l * LANES : (l + 1) * LANES])
            for l in range(blocks)
        ]

    def step_pair(sa, sb):
        for s in (sa, sb):
            step = softplus(
                jnp.dot(normed_ref[...], dtwall_ref[s], preferred_element_type=F32)
                + par_ref[s, states : states + 1, :]
            )
            step_ref[s] = step.reshape(rows // 8, 8, chans)
            drive_ref[s] = (step * xc_ref[s].astype(F32)).reshape(rows // 8, 8, chans)
            total = jnp.sum(step, axis=0, keepdims=True)
            for l in range(blocks):
                sums_ref[s, l : l + 1] = total[:, l * LANES : (l + 1) * LANES]
        pieces = [(s, l) for s in (sa, sb) for l in range(blocks)]
        rates = rates_of(sa) + rates_of(sb)

        def advance(group, held):
            held = list(held)
            for r in range(8):
                b_now = b_ref[group * 8 + r]
                for i, (s, l) in enumerate(pieces):
                    at = slice(l * LANES, (l + 1) * LANES)
                    decay = jnp.exp2(step_ref[s, group, r : r + 1, at] * rates[i])
                    held[i] = decay * held[i] + b_now * drive_ref[s, group, r : r + 1, at]
            return tuple(held)

        zero = jnp.zeros((states, LANES), F32)
        held = lax.fori_loop(0, rows // 8, advance, tuple(zero for _ in pieces))
        for i, (s, l) in enumerate(pieces):
            ends_ref[s, :, l * LANES : (l + 1) * LANES] = held[i].astype(BF16)

    def ends_copies(s, me):
        return (
            pltpu.make_async_remote_copy(
                src_ref=ends_ref.at[s], dst_ref=heldends_ref.at[me],
                send_sem=ends_sem.at[0, s], recv_sem=ends_sem.at[1, me],
                device_id={"seq": s}, device_id_type=mesh_id,
            ),
            pltpu.make_async_remote_copy(
                src_ref=sums_ref.at[s], dst_ref=heldsums_ref.at[me],
                send_sem=sums_sem.at[0, s], recv_sem=sums_sem.at[1, me],
                device_id={"seq": s}, device_id_type=mesh_id,
            ),
        )

    def send_ends(m):
        def body(p, carry):
            for j, s in enumerate(pair(m, p)):
                def go():
                    for copy in ends_copies(s, seq):
                        copy.start()
                if j == 0 and m == 0:
                    pl.when(p > 0)(go)
                else:
                    go()
            return carry

        lax.fori_loop(0, ny // 2, body, 0)

    def step_group(m):
        def body(p, carry):
            sa, sb = pair(m, p)
            for j, s in enumerate((sa, sb)):
                if j == 0 and m == 0:
                    @pl.when(p > 0)
                    def _():
                        sibling_wait(DTW, s)
                else:
                    sibling_wait(DTW, s)
            step_pair(sa, sb)
            return carry

        lax.fori_loop(0, ny // 2, body, 0)

    for m in range(nz + 1):
        both(lambda r: r.piece((DTW,), m))
        if m > 1:
            send_ends(m - 2)
        if m > 0:
            step_group(m - 1)
    spread(c_ref, bc_ref[states:])
    send_ends(nz - 1)
    heldends_ref[seq] = ends_ref[seq]
    heldsums_ref[seq] = sums_ref[seq]

    rates_own = [
        -LOG2E * jnp.exp(alog_ref[:, l * LANES : (l + 1) * LANES]) for l in range(blocks)
    ]

    def link(i, held):
        @pl.when(i != seq)
        def _():
            for copy in ends_copies(i, i):
                copy.wait_recv()
        out = []
        for l in range(blocks):
            at = slice(l * LANES, (l + 1) * LANES)
            back_ref[i, :, at] = held[l].astype(BF16)
            decay = jnp.exp2(heldsums_ref[i, l : l + 1] * rates_own[l])
            out.append(decay * held[l] + heldends_ref[i, :, at].astype(F32))
        return tuple(out)

    zero = jnp.zeros((states, LANES), F32)
    lax.fori_loop(0, count, link, tuple(zero for _ in range(blocks)))

    def back_copy(s, me):
        return pltpu.make_async_remote_copy(
            src_ref=back_ref.at[s], dst_ref=starts_ref.at[me],
            send_sem=back_sem.at[0, s], recv_sem=back_sem.at[1, me],
            device_id={"seq": s}, device_id_type=mesh_id,
        )

    def send_back(k, carry):
        m, j = k // ny, lax.rem(k, ny)
        dz = jnp.where(lax.rem(m, 2) == 1, -((m + 1) // 2), m // 2)
        dy = jnp.where(lax.rem(j, 2) == 1, -((j + 1) // 2), j // 2)
        back_copy(place(y - dy, z - dz), seq).start()
        return carry

    lax.fori_loop(1, count, send_back, 0)
    starts_ref[seq] = back_ref[seq]

    def out_copy(s):
        at = pl.ds(pl.multiple_of(s * chans, chans), chans)
        return pltpu.make_async_copy(out_ref.at[s], out_hbm.at[:, at], store_sem.at[s])

    def scan_pair(k, carry):
        m, p = k // (ny // 2), lax.rem(k, ny // 2)
        sa, sb = pair(m, p)

        @pl.when(k > 0)
        def _():
            for s in pair((k - 1) // (ny // 2), lax.rem(k - 1, ny // 2)):
                out_copy(s).start()
            back_copy(sa, sa).wait_recv()

        back_copy(sb, sb).wait_recv()
        pieces = [(s, l) for s in (sa, sb) for l in range(blocks)]
        rates = rates_of(sa) + rates_of(sb)

        def advance(group, held):
            held = list(held)
            for r in range(8):
                t = group * 8 + r
                b_now = b_ref[t]
                c_now = c_ref[t]
                for i, (s, l) in enumerate(pieces):
                    at = slice(l * LANES, (l + 1) * LANES)
                    decay = jnp.exp2(step_ref[s, group, r : r + 1, at] * rates[i])
                    held[i] = decay * held[i] + b_now * drive_ref[s, group, r : r + 1, at]
                    seen = c_now * held[i]
                    part_ref[i, pl.ds(pl.multiple_of(t * 8, 8), 8), :] = seen[:8] + seen[8:]
            return tuple(held)

        held = tuple(
            starts_ref[s, :, l * LANES : (l + 1) * LANES].astype(F32) for s, l in pieces
        )
        lax.fori_loop(0, rows // 8, advance, held)
        for i, (s, l) in enumerate(pieces):
            at = slice(l * LANES, (l + 1) * LANES)
            total = part_ref[i, pl.ds(0, rows, stride=8), :]
            for r in range(1, 8):
                total = total + part_ref[i, pl.ds(r, rows, stride=8), :]
            skip = par_ref[s, states + 1 : states + 2, at]
            y_out = (total + skip * xc_ref[s, :, at].astype(F32)).astype(BF16).astype(F32)
            wide = pl.ds(pl.multiple_of(s * chans + l * LANES, LANES), LANES)
            gate = gate_ref[:, wide].astype(F32)
            out_ref[s, :, at] = (y_out * silu(gate)).astype(BF16)
        return carry

    pairs = count // 2
    lax.fori_loop(0, pairs, scan_pair, 0)
    both(lambda r: r.drain())
    halo.wait_send()

    def finish(k, carry):
        s = lax.rem(seq + k, count)
        for copy in ends_copies(s, s):
            copy.wait_send()
        back_copy(s, s).wait_send()
        return carry

    lax.fori_loop(1, count, finish, 0)
    for s in pair((pairs - 1) // (ny // 2), (pairs - 1) % (ny // 2)):
        out_copy(s).start()

    def stored(s, carry):
        out_copy(s).wait()
        return carry

    lax.fori_loop(0, count, stored, 0)


def local(
    conv_input,
    gate_input,
    conv_weight,
    conv_bias,
    x_weight,
    dt_gain,
    dt_weight,
    dt_bias,
    a_log,
    skip,
):
    width = conv_weight.shape[0]
    rank = dt_weight.shape[0]
    states, chans = a_log.shape
    rows, inner = conv_input.shape
    count = lax.axis_size("seq")
    ny, nz = 4, count // 4
    par_rows = 32
    xw_rows = rank + 2 * states
    dma = pltpu.SemaphoreType.DMA
    vmem = pl.BlockSpec(memory_space=pltpu.VMEM)
    hbm = pl.BlockSpec(memory_space=pl.ANY)
    return pl.pallas_call(
        functools.partial(mixer_kernel, ny, nz),
        in_specs=[hbm, hbm] + [vmem] * 9,
        out_specs=hbm,
        out_shape=jax.ShapeDtypeStruct((rows, inner), BF16),
        scratch_shapes=[
            pltpu.VMEM((rows, inner), BF16),
            pltpu.VMEM((rows, inner), BF16),
            pltpu.VMEM((count, rows, chans), BF16),
            pltpu.VMEM((4, inner), BF16),
            pltpu.VMEM((par_rows, chans), F32),
            pltpu.VMEM((xw_rows, chans), BF16),
            pltpu.VMEM((count, par_rows, chans), F32),
            pltpu.VMEM((count, xw_rows, chans), BF16),
            pltpu.VMEM((count, rank, chans), BF16),
            pltpu.VMEM((count, rows, chans), BF16),
            pltpu.VMEM((rows, rank), F32),
            pltpu.VMEM((2 * states, rows), F32),
            pltpu.VMEM((rows, rank), BF16),
            pltpu.VMEM((rows, states, LANES), F32),
            pltpu.VMEM((rows, states, LANES), F32),
            pltpu.VMEM((count, rows // 8, 8, chans), F32),
            pltpu.VMEM((count, rows // 8, 8, chans), F32),
            pltpu.VMEM((2 * chans // LANES, rows * 8, LANES), F32),
            pltpu.VMEM((count, states, chans), BF16),
            pltpu.VMEM((count, chans // LANES, LANES), F32),
            pltpu.VMEM((count, states, chans), BF16),
            pltpu.VMEM((count, chans // LANES, LANES), F32),
            pltpu.VMEM((count, states, chans), BF16),
            pltpu.VMEM((count, states, chans), BF16),
            dma((2,)),
            dma((count,)),
            dma((2,)),
            dma((6 * (count - 1),)),
            dma((3, count)),
            dma((3, count)),
            dma((2, count)),
            dma((2, count)),
            dma((2, count)),
        ],
        compiler_params=pltpu.CompilerParams(
            collective_id=0, has_side_effects=True, vmem_limit_bytes=VMEM_LIMIT
        ),
        name="mixer",
    )(
        conv_input,
        gate_input,
        conv_weight,
        conv_bias[None, :],
        x_weight,
        dt_gain[None, :],
        dt_weight,
        dt_bias[None, :],
        a_log,
        skip[None, :],
        conv_input[rows - 4 :],
    )


def solution(mesh):
    return jax.shard_map(
        local,
        mesh=mesh,
        in_specs=(
            P(("batch", "seq"), None),
            P(("batch", "seq"), None),
            P(None, "seq"),
            P("seq"),
            P("seq", None),
            P(),
            P(None, "seq"),
            P("seq"),
            P(None, "seq"),
            P("seq"),
        ),
        out_specs=P(("batch", "seq"), None),
        check_vma=False,
    )
```

time: 667 us -> 127 us (0.19); the launches traced: 658 us -> 125 us
  local copies, waits for them, and re-layouts: 226 us -> 7.6 us
  other arithmetic: 167 us -> 0 us
  waiting for transfers between devices: 149 us -> 0 us
  Pallas kernels: 0 us -> 118 us
  blocking collectives: 52.1 us -> 0 us
  starting transfers between devices: 34.2 us -> 0 us
  between operations: 15.2 us -> 0.01 us
  matrix products: 13.1 us -> 0 us
    all_gather x2 -> x0, waiting for transfers between devices: 147 us -> none  [the longest x1 88 us: local(): proj = lax.all_gather(local_proj, 'seq', axis=0, tiled=True)]
    pallas_call x0 -> x1, Pallas kernels: none -> 118 us  [local(): pl.pallas_call(functools.partial(mixer_kernel, ny, nz), in_specs=[hbm, hb...]
    pad x12 -> x0, local copies, waits for them, and re-layouts: 99.8 us -> none  [selective_scan(): _, through = lax.associative_scan(link_blocks, (totals, state), axis=0)]
    reduce_sum x11 -> x0, other arithmetic: 94.6 us -> none  [the longest x8 74.5 us: selective_scan(): local_parts.append(jnp.sum(c_now[:, :, None] * state, axis=1))]
    slice x15 -> x1, local copies, waits for them, and re-layouts: 56.2 us -> 1.56 us  [local(): conv_input[rows - 4:]]
    all_to_all x1 -> x0, blocking collectives: 52.1 us -> none  [local(): return lax.all_to_all(gated, 'seq', split_axis=0, concat_axis=1, tiled=True)]
    unnamed x267 -> x2, local copies, waits for them, and re-layouts: 46.1 us -> 4.82 us
    all_to_all x3 -> x0, starting transfers between devices: 30.8 us -> none  [the longest x1 11.7 us: from_everyone(): return lax.all_to_all(copies, axis, split_axis=0, concat_axis=0, tiled=True)]
  transfers between devices with their start and end apart: 6 -> 0, of which waited for: 3 -> 0; matrix products, arithmetic and copies ran while one was open for 60% -> 0% of each run, Pallas kernels for 0% -> 0%
where the time goes in v2:
time: 127 us; the launch traced here: 125 us
  Pallas kernels  118 us (93%)
  local copies, waits for them, and re-layouts  7.6 us (6%)
    pallas_call x1, Pallas kernels, local(): pl.pallas_call(functools.partial(mixer_kernel, ny, nz), in_specs=[hbm, hb...  118 us
    unnamed x2, local copies, waits for them, and re-layouts  4.82 us

profile of v2, /device:TPU:8, one launch (start us, length us, event | category | flops | bytes accessed | tf_op | source)
XLA Modules:
  0.0 125.3 jit_solution(6000483235864981636)
XLA Ops:
  0.0 1.2 broadcast_in_dim.12.cb_ref
  1.2 1.6 %slice.3.halo_ref = bf16[4,8192]{1,0:T(4,128)(2,1)} slice(bf16[128,8192]{1,0:T(8,128)(2,1)} %x_hbm.1), slice={[124:128], [0:8192]} | slice | bytes 131072 | tf_op jit(solution)/shard_map/slice | solution.py:591
  2.8 1.7 %copy.11.xw_ref = bf16[256,288]{1,0:T(8,128)(2,1)} copy(bf16[256,288]{0,1:T(8,128)(2,1)} %param.14) | data formatting | bytes 294912 | tf_op args[4]
  4.5 117.7 %mixer.1 = bf16[128,8192]{1,0:T(8,128)(2,1)} custom-call(bf16[128,8192]{1,0:T(8,128)(2,1)} %x_hbm.1, bf16[128,8192]{1,0:T(8,128)(2,1)} %gate_hbm.1, bf16[4,256]{1,0:T(4,128)(2,1)} %cw_ref.1, bf16[1,256]{1,0:T(2,128)(2,1)} %broadcast_in_dim.12.cb_ref, bf16[256,288]{1,0:T(8,128)(2,1)} %copy.11.xw_ref, f32[1,256]{1,0:T(1,128)} %bitcast.3, ...), custom_call_target="tpu_custom_call" | custom-call | tf_op jit(solution)/shard_map/mixer/pallas_call | solution.py:536
  122.2 3.1 %copy.13 = bf16[128,8192]{1,0:T(8,128)(2,1)} copy(bf16[128,8192]{1,0:T(8,128)(2,1)} %mixer.1) | data formatting | bytes 4194304

commit v3 on v2

v3 whole, which is shorter than its diff:
```python
import functools

import jax
import jax.numpy as jnp
from jax import lax
from jax.experimental import pallas as pl
from jax.experimental.pallas import tpu as pltpu
from jax.sharding import PartitionSpec as P

LOG2E = 1.4426950408889634
LANES = 128
F32 = jnp.float32
BF16 = jnp.bfloat16
VMEM_LIMIT = 60 * 1024 * 1024
PAR, XW, DTW = 0, 1, 2


def silu(v):
    return v / (1.0 + jnp.exp(-v))


def softplus(v):
    return jnp.maximum(v, 0.0) + jnp.log1p(jnp.exp(-jnp.abs(v)))


def spread(table_ref, turned):
    count, rows = turned.shape
    for t in range(rows):
        table_ref[t] = jnp.broadcast_to(turned[:, t : t + 1], (count, LANES))


def zigzag(j):
    return -(j + 1) // 2 if j % 2 else j // 2


class Route:
    def __init__(self, first, second, where, h, owns, outs, send_sem, recv_sem, sib_sem, sibling,
                 offer, quarter):
        self.offer, self.quarter = offer, quarter
        self.first, self.second, self.where, self.h = first, second, where, h
        self.owns, self.outs = owns, outs
        self.send_sem, self.recv_sem, self.sib_sem = send_sem, recv_sem, sib_sem
        self.sibling = sibling
        self.sent = []
        self.reach = {1: first // 2, -1: first - 1 - first // 2}

    def span(self, part):
        rows = self.outs[part].shape[1]
        if part == DTW:
            size = rows // 8
            return pl.ds(pl.multiple_of(self.h * (rows // 2) + self.quarter * size, size), size)
        return pl.ds(self.h * (rows // 2), rows // 2)

    def target(self, part, fo, so):
        return self.outs[part].at[self.where(fo, so), self.span(part)]

    def source(self, part, fo, so):
        if fo == 0 and so == 0:
            return self.owns[part].at[self.span(part)]
        return self.target(part, fo, so)

    def send(self, part, fo, so, sem, device):
        pltpu.make_async_remote_copy(
            src_ref=self.source(part, fo, so),
            dst_ref=self.target(part, fo, so),
            send_sem=self.send_sem.at[len(self.sent)],
            recv_sem=sem.at[part, self.where(fo, so)],
            device_id=device,
            device_id_type=pl.DeviceIdType.MESH,
        ).start()
        self.sent.append(part)

    def push(self, part, fo, so, df, ds):
        self.send(part, fo, so, self.recv_sem, {"seq": self.where(df, ds)})

    def share(self, part, fo, so):
        if part == DTW:
            self.offer(self.target(part, fo, so), self.where(fo, so))
            return
        self.send(part, fo, so, self.sib_sem, {"batch": self.sibling})

    def arrive(self, part, fo, so):
        pltpu.make_async_remote_copy(
            src_ref=self.target(part, fo, so),
            dst_ref=self.target(part, fo, so),
            send_sem=self.send_sem.at[0],
            recv_sem=self.recv_sem.at[part, self.where(fo, so)],
            device_id={"batch": self.sibling},
            device_id_type=pl.DeviceIdType.MESH,
        ).wait_recv()

    def drain(self):
        for i, part in enumerate(self.sent):
            pltpu.make_async_remote_copy(
                src_ref=self.target(part, 0, 0),
                dst_ref=self.target(part, 0, 0),
                send_sem=self.send_sem.at[i],
                recv_sem=self.recv_sem.at[part, self.where(0, 0)],
                device_id={"batch": self.sibling},
                device_id_type=pl.DeviceIdType.MESH,
            ).wait_send()

    def straight(self, ring):
        return [zigzag(j) for j in range(1, ring)]


class ZFirst(Route):
    def launch(self, part, fo):
        for so in self.straight(self.second):
            self.push(part, fo, 0, 0, so)

    def open(self, parts):
        for part in parts:
            for way in (1, -1):
                self.push(part, 0, 0, way, 0)
            self.launch(part, 0)

    def round(self, parts, r):
        for part in parts:
            for way in (1, -1):
                if r <= self.reach[way]:
                    self.arrive(part, -way * r, 0)
                    if r < self.reach[way]:
                        self.push(part, -way * r, 0, way, 0)
                    self.launch(part, -way * r)
                    self.share(part, -way * r, 0)
        for part in parts:
            for fo in [zigzag(j) for j in range(self.first)]:
                if abs(fo) == r - 1:
                    for so in self.straight(self.second):
                        self.arrive(part, fo, so)
                        self.share(part, fo, so)


class YFirst(Route):
    def far(self, fo, way):
        longer = self.second // 2 if fo % 2 == 0 else self.second - 1 - self.second // 2
        return longer if way == 1 else self.second - 1 - longer

    def launch(self, part, fo):
        for way in (1, -1):
            self.push(part, fo, 0, 0, way)

    def open(self, parts):
        for part in parts:
            for fo in self.straight(self.first):
                self.push(part, 0, 0, fo, 0)
            self.launch(part, 0)

    def round(self, parts, r):
        if r == 1:
            for part in parts:
                for fo in self.straight(self.first):
                    self.arrive(part, fo, 0)
                    self.launch(part, fo)
                    self.share(part, fo, 0)
        for part in parts:
            for fo in [zigzag(j) for j in range(self.first)]:
                for way in (1, -1):
                    if r <= self.far(fo, way):
                        self.arrive(part, fo, -way * r)
                        if r < self.far(fo, way):
                            self.push(part, fo, -way * r, 0, way)
                        self.share(part, fo, -way * r)


def mixer_kernel(ny, nz, x_hbm, gate_hbm, cw_ref, cb_ref, xw_ref, gain_ref, dtw_ref, dtb_ref,
                 alog_ref, skip_ref, out_hbm,
                 tail_ref, halo_ref, x_ref, gate_ref, gated_ref, out_ref, prior_ref, parown_ref, par_ref, xwall_ref,
                 dtwall_ref, xc_ref, rate_ref, proj_ref, normed_ref, b_ref, c_ref, step_ref,
                 drive_ref, part_ref, ends_ref, sums_ref, heldends_ref, heldsums_ref, back_ref,
                 starts_ref,
                 load_sem, store_sem, halo_sem, send_sem, recv_sem, sib_sem, across_sem, hand_sem,
                 ends_sem, sums_sem, back_sem):
    count = ny * nz
    rows, inner = x_ref.shape
    width = cw_ref.shape[0]
    states, chans = alog_ref.shape
    rank = normed_ref.shape[1]
    taps = states + 2
    seq = lax.axis_index("seq")
    batch = lax.axis_index("batch")
    core = lax.rem(batch, 2)
    y, z = seq // nz, lax.rem(seq, nz)
    sibling = batch + 1 - 2 * core
    mesh_id = pl.DeviceIdType.MESH
    slab = batch // 2
    slabs = lax.axis_size("batch") // 2

    def beside(d):
        return lax.rem(slab + d, slabs) * 2 + core

    def place(yy, zz):
        return lax.rem(yy + ny, ny) * nz + lax.rem(zz + nz, nz)

    load_x = pltpu.make_async_copy(x_hbm, x_ref, load_sem.at[0])
    load_gate = pltpu.make_async_copy(gate_hbm, gate_ref, load_sem.at[1])
    load_tail = pltpu.make_async_copy(x_hbm.at[pl.ds(rows - 16, 16)], tail_ref, load_sem.at[2])
    load_tail.start()
    load_x.start()
    load_gate.start()

    barrier = pltpu.get_barrier_semaphore()
    after, before = lax.rem(seq + 1, count), lax.rem(seq + count - 1, count)
    for there in (place(y + 1, z), place(y - 1, z), place(y + 2, z), place(y, z + 1),
                  place(y, z - 1), after, before):
        pl.semaphore_signal(barrier, inc=1, device_id={"seq": there}, device_id_type=mesh_id)
    for there in (sibling, *(beside(d) for d in range(1, slabs))):
        pl.semaphore_signal(barrier, inc=1, device_id={"batch": there}, device_id_type=mesh_id)

    parown_ref[...] = jnp.zeros_like(parown_ref)
    parown_ref[:states] = alog_ref[...]
    parown_ref[states : states + 1] = dtb_ref[...]
    parown_ref[states + 1 : states + 2] = skip_ref[...]
    parown_ref[taps : taps + width] = cw_ref[...].astype(F32)
    parown_ref[taps + width : taps + width + 1] = cb_ref[...].astype(F32).reshape(1, chans)
    owns, outs = (parown_ref, xw_ref, dtw_ref), (par_ref, xwall_ref, dtwall_ref)
    proj_ref[...] = jnp.zeros_like(proj_ref)
    for part in (PAR, XW, DTW):
        outs[part][seq] = owns[part][...]

    load_tail.wait()
    halo_ref[...] = tail_ref[...].astype(F32)[16 - halo_ref.shape[0] :].astype(BF16)
    pl.semaphore_wait(barrier, 8 + slabs - 1)

    def across(ref, at, d):
        return pltpu.make_async_remote_copy(
            src_ref=ref, dst_ref=ref, send_sem=across_sem.at[0, d - 1, at],
            recv_sem=across_sem.at[1, d - 1, at], device_id={"batch": beside(d)},
            device_id_type=mesh_id,
        )

    def offer(ref, at):
        for d in range(1, slabs):
            across(ref, at, d).start()

    shared = (owns, outs, send_sem, recv_sem, sib_sem, sibling, offer, slab)
    routes = (
        ZFirst(nz, ny, lambda fo, so: place(y + so, z + fo), 0, *shared),
        YFirst(ny, nz, lambda fo, so: place(y + fo, z + so), 1, *shared),
    )

    def both(act):
        for h in range(2):
            @pl.when(core == h)
            def _():
                act(routes[h])

    halo = pltpu.make_async_remote_copy(
        src_ref=halo_ref, dst_ref=prior_ref, send_sem=halo_sem.at[0], recv_sem=halo_sem.at[1],
        device_id={"seq": after}, device_id_type=mesh_id,
    )
    both(lambda r: r.open((DTW, PAR, XW)))
    halo.start()
    load_gate.wait()

    def silu_gate(i, carry):
        at = pl.ds(pl.multiple_of(i * chans, chans), chans)
        gated_ref[i] = silu(gate_ref[:, at].astype(F32))
        return carry

    lax.fori_loop(0, count, silu_gate, 0)
    load_x.wait()
    halo.wait_recv()

    def sibling_wait(part, at):
        size = outs[part].shape[1] // 2
        dst = outs[part].at[at, pl.ds(pl.multiple_of((1 - core) * size, size), size)]
        pltpu.make_async_remote_copy(
            src_ref=dst, dst_ref=dst, send_sem=send_sem.at[0], recv_sem=sib_sem.at[part, at],
            device_id={"batch": sibling}, device_id_type=mesh_id,
        ).wait_recv()

    first_rows = jnp.where(seq > 0, 1.0, 0.0)

    def conv_shard(s):
        at = pl.ds(pl.multiple_of(s * chans, chans), chans)
        prior = prior_ref[:, at].astype(F32) * first_rows
        full = jnp.concatenate([jnp.zeros_like(prior), prior, x_ref[:, at].astype(F32)], 0)
        lead = 2 * prior.shape[0] - (width - 1)
        total = jnp.broadcast_to(par_ref[s, taps + width : taps + width + 1, :], (rows, chans))
        for tap in range(width):
            total = total + par_ref[s, taps + tap : taps + tap + 1, :] * full[
                lead + tap : lead + tap + rows
            ]
        xc = silu(total).astype(BF16)
        xc_ref[s] = xc
        rate_ref[s] = -LOG2E * jnp.exp(par_ref[s, :states])
        proj_ref[...] += lax.dot_general(
            xwall_ref[s], xc, (((1,), (1,)), ((), ())), preferred_element_type=F32
        )

    def pair(m, p):
        dz = jnp.where(lax.rem(m, 2) == 1, -((m + 1) // 2), m // 2)
        return place(y + p, z + dz), place(y - p - 1 + ny, z + dz)

    def kin(m, kind):
        dz = jnp.where(lax.rem(m, 2) == 1, -((m + 1) // 2), m // 2)
        same = lax.rem(y, 2) == kind
        return (place(y + jnp.where(same, 0, -1), z + dz),
                place(y + jnp.where(same, -2, 1), z + dz))

    def conv_group(m):
        def body(p, carry):
            sa, sb = pair(m, p)
            for j, s in enumerate((sa, sb)):
                if j == 0 and m == 0:
                    @pl.when(p > 0)
                    def _():
                        sibling_wait(PAR, s)
                        sibling_wait(XW, s)
                else:
                    sibling_wait(PAR, s)
                    sibling_wait(XW, s)
            conv_shard(sa)
            conv_shard(sb)
            return carry

        lax.fori_loop(0, ny // 2, body, 0)

    rounds = nz // 2 + 1
    groups = [[m for m in range(nz) if abs(zigzag(m)) == r - 1] for r in range(1, rounds + 1)]
    eighth = rank // 8

    def hand_over(m):
        def body(k, carry):
            sa, sb = pair(m, k // 2)
            at = jnp.where(lax.rem(k, 2) == 0, sa, sb)

            def go():
                for d in range(1, slabs):
                    there = lax.rem(slab - d + slabs, slabs)
                    dst = dtwall_ref.at[at, pl.ds(
                        pl.multiple_of(core * (rank // 2) + there * eighth, eighth), eighth)]
                    across(dst, at, d).wait_recv()
                hand(at).start()

            if m == 0:
                pl.when(k > 0)(go)
            else:
                go()
            return carry

        lax.fori_loop(0, ny, body, 0)

    def hand(at):
        half = dtwall_ref.at[at, pl.ds(pl.multiple_of(core * (rank // 2), rank // 2), rank // 2)]
        return pltpu.make_async_remote_copy(
            src_ref=half, dst_ref=half, send_sem=hand_sem.at[at], recv_sem=sib_sem.at[DTW, at],
            device_id={"batch": sibling}, device_id_type=mesh_id,
        )

    for r in range(1, rounds + 1):
        both(lambda route: route.round((DTW, PAR, XW), r))
        for m in groups[r - 1]:
            conv_group(m)
    hand_over(0)

    low = proj_ref[:rank]
    mean = jnp.mean(low * low, axis=0, keepdims=True)
    normed_ref[...] = ((low * lax.rsqrt(mean + 1e-06)).T * gain_ref[...]).astype(BF16)
    spread(b_ref, proj_ref[rank : rank + states])

    span = 16
    blocks = chans // LANES

    def rates_of(s):
        return [rate_ref[s, :, l * LANES : (l + 1) * LANES] for l in range(blocks)]

    def step_pair(sa, sb):
        for s in (sa, sb):
            step = softplus(
                jnp.dot(normed_ref[...], dtwall_ref[s], preferred_element_type=F32)
                + par_ref[s, states : states + 1, :]
            )
            step_ref[s] = step.reshape(rows // 8, 8, chans)
            drive_ref[s] = (step * xc_ref[s].astype(F32)).reshape(rows // 8, 8, chans)
            total = jnp.sum(step, axis=0, keepdims=True)
            for l in range(blocks):
                sums_ref[s, l : l + 1] = total[:, l * LANES : (l + 1) * LANES]
        pieces = [(s, l) for s in (sa, sb) for l in range(blocks)]
        rates = rates_of(sa) + rates_of(sb)

        def advance(g, held):
            held = list(held)
            for r in range(span):
                b_now = b_ref[g * span + r]
                group = g * (span // 8) + r // 8
                row = slice(r % 8, r % 8 + 1)
                for i, (s, l) in enumerate(pieces):
                    at = slice(l * LANES, (l + 1) * LANES)
                    decay = jnp.exp2(step_ref[s, group, row, at] * rates[i])
                    held[i] = decay * held[i] + b_now * drive_ref[s, group, row, at]
            return tuple(held)

        zero = jnp.zeros((states, LANES), F32)
        held = lax.fori_loop(0, rows // span, advance, tuple(zero for _ in pieces))
        for i, (s, l) in enumerate(pieces):
            ends_ref[s, :, l * LANES : (l + 1) * LANES] = held[i].astype(BF16)

    def ends_copies(s, me):
        return (
            pltpu.make_async_remote_copy(
                src_ref=ends_ref.at[s], dst_ref=heldends_ref.at[me],
                send_sem=ends_sem.at[0, s], recv_sem=ends_sem.at[1, me],
                device_id={"seq": s}, device_id_type=mesh_id,
            ),
            pltpu.make_async_remote_copy(
                src_ref=sums_ref.at[s], dst_ref=heldsums_ref.at[me],
                send_sem=sums_sem.at[0, s], recv_sem=sums_sem.at[1, me],
                device_id={"seq": s}, device_id_type=mesh_id,
            ),
        )

    def send_ends(m, kind):
        for s in kin(m, kind):
            @pl.when(s != seq)
            def _():
                for copy in ends_copies(s, seq):
                    copy.start()

    def step_kin(m, kind):
        sa, sb = kin(m, kind)
        for s in (sa, sb):
            @pl.when(s != seq)
            def _():
                sibling_wait(DTW, s)
        step_pair(sa, sb)

    rates_own = rates_of(seq)

    def link(i, held):
        @pl.when(i != seq)
        def _():
            for copy in ends_copies(i, i):
                copy.wait_recv()
        out = []
        for l in range(blocks):
            at = slice(l * LANES, (l + 1) * LANES)
            back_ref[i, :, at] = held[l].astype(BF16)
            decay = jnp.exp2(heldsums_ref[i, l : l + 1] * rates_own[l])
            out.append(decay * held[l] + heldends_ref[i, :, at].astype(F32))
        return tuple(out)

    def back_copy(s, me):
        return pltpu.make_async_remote_copy(
            src_ref=back_ref.at[s], dst_ref=starts_ref.at[me],
            send_sem=back_sem.at[0, s], recv_sem=back_sem.at[1, me],
            device_id={"seq": s}, device_id_type=mesh_id,
        )

    def send_back(k, carry):
        m, j = k // ny, lax.rem(k, ny)
        dz = jnp.where(lax.rem(m, 2) == 1, -((m + 1) // 2), m // 2)
        dy = jnp.where(lax.rem(j, 2) == 1, -((j + 1) // 2), j // 2)
        back_copy(place(y - dy, z - dz), seq).start()
        return carry

    def prefix():
        heldends_ref[seq] = ends_ref[seq]
        heldsums_ref[seq] = sums_ref[seq]
        zero = jnp.zeros((states, LANES), F32)
        lax.fori_loop(0, count, link, tuple(zero for _ in range(blocks)))
        starts_ref[seq] = back_ref[seq]
        lax.fori_loop(1, count, send_back, 0)

    for m in range(nz):
        if m + 1 < nz:
            hand_over(m + 1)
        if m > 0:
            send_ends(m - 1, 0)
        step_kin(m, 0)

    def later_kin(m, carry):
        send_ends(jnp.where(m == 0, nz - 1, m - 1), jnp.where(m == 0, 0, 1))
        step_kin(m, 1)
        return carry

    lax.fori_loop(0, nz // 2, later_kin, 0)
    spread(c_ref, proj_ref[rank + states :])
    pl.when(lax.rem(y, 2) == 0)(prefix)
    lax.fori_loop(nz // 2, nz, later_kin, 0)
    send_ends(nz - 1, 1)

    def out_copy(s):
        at = pl.ds(pl.multiple_of(s * chans, chans), chans)
        return pltpu.make_async_copy(out_ref.at[s], out_hbm.at[:, at], store_sem.at[s])

    def scan_pair(k, carry):
        sa, sb = kin(lax.rem(k, nz), k // nz)

        @pl.when(k > 0)
        def _():
            for s in kin(lax.rem(k - 1, nz), (k - 1) // nz):
                out_copy(s).start()

        for s in (sa, sb):
            @pl.when(s != seq)
            def _():
                back_copy(s, s).wait_recv()

        pieces = [(s, l) for s in (sa, sb) for l in range(blocks)]
        rates = rates_of(sa) + rates_of(sb)

        def advance(g, held):
            held = list(held)
            for r in range(span):
                t = g * span + r
                b_now = b_ref[t]
                c_now = c_ref[t]
                group = g * (span // 8) + r // 8
                row = slice(r % 8, r % 8 + 1)
                for i, (s, l) in enumerate(pieces):
                    at = slice(l * LANES, (l + 1) * LANES)
                    decay = jnp.exp2(step_ref[s, group, row, at] * rates[i])
                    held[i] = decay * held[i] + b_now * drive_ref[s, group, row, at]
                    seen = c_now * held[i]
                    part_ref[i, group, pl.ds(r % 8, 8, stride=8), :] = seen[:8] + seen[8:]
            return tuple(held)

        held = tuple(
            starts_ref[s, :, l * LANES : (l + 1) * LANES].astype(F32) for s, l in pieces
        )
        lax.fori_loop(0, rows // span, advance, held)
        for i, (s, l) in enumerate(pieces):
            at = slice(l * LANES, (l + 1) * LANES)
            total = part_ref[i, :, :8, :]
            for k in range(1, 8):
                total = total + part_ref[i, :, k * 8 : (k + 1) * 8, :]
            skip = par_ref[s, states + 1 : states + 2, at]
            y_out = total.reshape(rows, LANES) + skip * xc_ref[s, :, at].astype(F32)
            y_out = y_out.astype(BF16).astype(F32)
            out_ref[s, :, at] = (y_out * gated_ref[s, :, at]).astype(BF16)
        return carry

    pairs = count // 2
    lax.fori_loop(0, 3, scan_pair, 0)
    pl.when(lax.rem(y, 2) == 1)(prefix)
    lax.fori_loop(3, pairs, scan_pair, 0)
    both(lambda r: r.drain())
    halo.wait_send()

    def finish(k, carry):
        s = lax.rem(seq + k, count)
        for copy in ends_copies(s, s):
            copy.wait_send()
        back_copy(s, s).wait_send()
        hand(s).wait_send()
        small = dtwall_ref.at[s, pl.ds(0, eighth)]
        for d in range(1, slabs):
            across(small, s, d).wait_send()
        return carry

    lax.fori_loop(1, count, finish, 0)
    for s in kin(nz - 1, 1):
        out_copy(s).start()

    def stored(s, carry):
        out_copy(s).wait()
        return carry

    lax.fori_loop(0, count, stored, 0)


def local(
    conv_input,
    gate_input,
    conv_weight,
    conv_bias,
    x_weight,
    dt_gain,
    dt_weight,
    dt_bias,
    a_log,
    skip,
):
    width = conv_weight.shape[0]
    rank = dt_weight.shape[0]
    states, chans = a_log.shape
    rows, inner = conv_input.shape
    count = lax.axis_size("seq")
    ny, nz = 4, count // 4
    par_rows = 32
    xw_rows = rank + 2 * states
    dma = pltpu.SemaphoreType.DMA
    vmem = pl.BlockSpec(memory_space=pltpu.VMEM)
    hbm = pl.BlockSpec(memory_space=pl.ANY)
    return pl.pallas_call(
        functools.partial(mixer_kernel, ny, nz),
        in_specs=[hbm, hbm] + [vmem] * 8,
        out_specs=hbm,
        out_shape=jax.ShapeDtypeStruct((rows, inner), BF16),
        scratch_shapes=[
            pltpu.VMEM((16, inner), BF16),
            pltpu.VMEM((4, inner), BF16),
            pltpu.VMEM((rows, inner), BF16),
            pltpu.VMEM((rows, inner), BF16),
            pltpu.VMEM((count, rows, chans), F32),
            pltpu.VMEM((count, rows, chans), BF16),
            pltpu.VMEM((4, inner), BF16),
            pltpu.VMEM((par_rows, chans), F32),
            pltpu.VMEM((count, par_rows, chans), F32),
            pltpu.VMEM((count, xw_rows, chans), BF16),
            pltpu.VMEM((count, rank, chans), BF16),
            pltpu.VMEM((count, rows, chans), BF16),
            pltpu.VMEM((count, states, chans), F32),
            pltpu.VMEM((xw_rows, rows), F32),
            pltpu.VMEM((rows, rank), BF16),
            pltpu.VMEM((rows, states, LANES), F32),
            pltpu.VMEM((rows, states, LANES), F32),
            pltpu.VMEM((count, rows // 8, 8, chans), F32),
            pltpu.VMEM((count, rows // 8, 8, chans), F32),
            pltpu.VMEM((2 * chans // LANES, rows // 8, 64, LANES), F32),
            pltpu.VMEM((count, states, chans), BF16),
            pltpu.VMEM((count, chans // LANES, LANES), F32),
            pltpu.VMEM((count, states, chans), BF16),
            pltpu.VMEM((count, chans // LANES, LANES), F32),
            pltpu.VMEM((count, states, chans), BF16),
            pltpu.VMEM((count, states, chans), BF16),
            dma((3,)),
            dma((count,)),
            dma((2,)),
            dma((6 * (count - 1),)),
            dma((3, count)),
            dma((3, count)),
            dma((2, 3, count)),
            dma((count,)),
            dma((2, count)),
            dma((2, count)),
            dma((2, count)),
        ],
        compiler_params=pltpu.CompilerParams(
            collective_id=0, has_side_effects=True, vmem_limit_bytes=VMEM_LIMIT
        ),
        name="mixer",
    )(
        conv_input,
        gate_input,
        conv_weight,
        conv_bias,
        x_weight.T,
        dt_gain[None, :],
        dt_weight,
        dt_bias[None, :],
        a_log,
        skip[None, :],
    )


def solution(mesh):
    return jax.shard_map(
        local,
        mesh=mesh,
        in_specs=(
            P(("batch", "seq"), None),
            P(("batch", "seq"), None),
            P(None, "seq"),
            P("seq"),
            P("seq", None),
            P(),
            P(None, "seq"),
            P("seq"),
            P(None, "seq"),
            P("seq"),
        ),
        out_specs=P(("batch", "seq"), None),
        check_vma=False,
    )
```

time: 127 us -> 96.3 us (0.76); the launches traced: 125 us -> 96.2 us
  Pallas kernels: 118 us -> 93.1 us
  local copies, waits for them, and re-layouts: 7.6 us -> 3.1 us
    pallas_call x1, Pallas kernels: 118 us -> 93.1 us  [local(): pl.pallas_call(functools.partial(mixer_kernel, ny, nz), in_specs=[hbm, hb...]
    unnamed x2 -> x1, local copies, waits for them, and re-layouts: 4.82 us -> 3.1 us
    slice x1 -> x0, local copies, waits for them, and re-layouts: 1.56 us -> none  [local(): conv_input[rows - 4:]]
where the time goes in v3:
time: 96.3 us; the launch traced here: 96.2 us
  Pallas kernels  93.1 us (97%)
  local copies, waits for them, and re-layouts  3.1 us (3%)
    pallas_call x1, Pallas kernels, local(): pl.pallas_call(functools.partial(mixer_kernel, ny, nz), in_specs=[hbm, hb...  93.1 us
    unnamed x1, local copies, waits for them, and re-layouts  3.1 us

profile of v3, /device:TPU:8, one launch (start us, length us, event | category | flops | bytes accessed | tf_op | source)
XLA Modules:
  0.0 96.2 jit_solution(15653833759903542561)
XLA Ops:
  0.0 93.1 %mixer.1 = bf16[128,8192]{1,0:T(8,128)(2,1)} custom-call(bf16[128,8192]{1,0:T(8,128)(2,1)} %x_hbm.1, bf16[128,8192]{1,0:T(8,128)(2,1)} %gate_hbm.1, bf16[4,256]{1,0:T(4,128)(2,1)} %cw_ref.1, bf16[256]{0:T(256)(128)(2,1)} %cb_ref.1, bf16[288,256]{1,0:T(8,128)(2,1)} %bitcast.4, f32[1,256]{1,0:T(1,128)} %bitcast.5, bf16[256,256]{1,0:T(8,128)(2,1)} %dtw_ref.1, ...), custom_call_target="tpu_custom_call" | custom-call | tf_op jit(solution)/shard_map/mixer/pallas_call | solution.py:588
  93.1 3.1 %copy.12 = bf16[128,8192]{1,0:T(8,128)(2,1)} copy(bf16[128,8192]{1,0:T(8,128)(2,1)} %mixer.1) | data formatting | bytes 4194304

commit v4 on v3

--- a/solution.py
+++ b/solution.py
@@ -100,6 +100,10 @@
                 device_id_type=pl.DeviceIdType.MESH,
             ).wait_send()
 
+    def end(self, part, fo, so):
+        self.arrive(part, fo, so)
+        self.share(part, fo, so)
+
     def straight(self, ring):
         return [zigzag(j) for j in range(1, ring)]
 
@@ -115,21 +119,25 @@
                 self.push(part, 0, 0, way, 0)
             self.launch(part, 0)
 
-    def round(self, parts, r):
+    def near(self, part, r, way):
+        self.arrive(part, -way * r, 0)
+        if r < self.reach[way]:
+            self.push(part, -way * r, 0, way, 0)
+        self.launch(part, -way * r)
+        self.share(part, -way * r, 0)
+
+    def events(self, parts, r):
+        found = []
         for part in parts:
             for way in (1, -1):
                 if r <= self.reach[way]:
-                    self.arrive(part, -way * r, 0)
-                    if r < self.reach[way]:
-                        self.push(part, -way * r, 0, way, 0)
-                    self.launch(part, -way * r)
-                    self.share(part, -way * r, 0)
+                    found.append(functools.partial(self.near, part, r, way))
         for part in parts:
             for fo in [zigzag(j) for j in range(self.first)]:
                 if abs(fo) == r - 1:
                     for so in self.straight(self.second):
-                        self.arrive(part, fo, so)
-                        self.share(part, fo, so)
+                        found.append(functools.partial(self.end, part, fo, so))
+        return found
 
 
 class YFirst(Route):
@@ -147,21 +155,29 @@
                 self.push(part, 0, 0, fo, 0)
             self.launch(part, 0)
 
-    def round(self, parts, r):
+    def near(self, part, fo):
+        self.arrive(part, fo, 0)
+        self.launch(part, fo)
+        self.share(part, fo, 0)
+
+    def along(self, part, fo, r, way):
+        self.arrive(part, fo, -way * r)
+        if r < self.far(fo, way):
+            self.push(part, fo, -way * r, 0, way)
+        self.share(part, fo, -way * r)
+
+    def events(self, parts, r):
+        found = []
         if r == 1:
             for part in parts:
                 for fo in self.straight(self.first):
-                    self.arrive(part, fo, 0)
-                    self.launch(part, fo)
-                    self.share(part, fo, 0)
+                    found.append(functools.partial(self.near, part, fo))
         for part in parts:
             for fo in [zigzag(j) for j in range(self.first)]:
                 for way in (1, -1):
                     if r <= self.far(fo, way):
-                        self.arrive(part, fo, -way * r)
-                        if r < self.far(fo, way):
-                            self.push(part, fo, -way * r, 0, way)
-                        self.share(part, fo, -way * r)
+                        found.append(functools.partial(self.along, part, fo, r, way))
+        return found
 
 
 def mixer_kernel(ny, nz, x_hbm, gate_hbm, cw_ref, cb_ref, xw_ref, gain_ref, dtw_ref, dtb_ref,
@@ -252,16 +268,12 @@
     )
     both(lambda r: r.open((DTW, PAR, XW)))
     halo.start()
-    load_gate.wait()
 
     def silu_gate(i, carry):
         at = pl.ds(pl.multiple_of(i * chans, chans), chans)
         gated_ref[i] = silu(gate_ref[:, at].astype(F32))
         return carry
 
-    lax.fori_loop(0, count, silu_gate, 0)
-    load_x.wait()
-    halo.wait_recv()
 
     def sibling_wait(part, at):
         size = outs[part].shape[1] // 2
@@ -300,23 +312,12 @@
         return (place(y + jnp.where(same, 0, -1), z + dz),
                 place(y + jnp.where(same, -2, 1), z + dz))
 
-    def conv_group(m):
-        def body(p, carry):
-            sa, sb = pair(m, p)
-            for j, s in enumerate((sa, sb)):
-                if j == 0 and m == 0:
-                    @pl.when(p > 0)
-                    def _():
-                        sibling_wait(PAR, s)
-                        sibling_wait(XW, s)
-                else:
-                    sibling_wait(PAR, s)
-                    sibling_wait(XW, s)
-            conv_shard(sa)
-            conv_shard(sb)
-            return carry
-
-        lax.fori_loop(0, ny // 2, body, 0)
+    def conv_pair(m, p):
+        for j, s in enumerate(pair(m, p)):
+            if m or p or j:
+                sibling_wait(PAR, s)
+                sibling_wait(XW, s)
+            conv_shard(s)
 
     rounds = nz // 2 + 1
     groups = [[m for m in range(nz) if abs(zigzag(m)) == r - 1] for r in range(1, rounds + 1)]
@@ -350,11 +351,31 @@
             device_id={"batch": sibling}, device_id_type=mesh_id,
         )
 
+    slots = 4
+    waiting = []
     for r in range(1, rounds + 1):
-        both(lambda route: route.round((DTW, PAR, XW), r))
-        for m in groups[r - 1]:
-            conv_group(m)
+        lists = [route.events((DTW, PAR, XW), r) for route in routes]
+        for q in range(slots):
+            for h in range(2):
+                mine = lists[h][len(lists[h]) * q // slots : len(lists[h]) * (q + 1) // slots]
+                if mine:
+                    @pl.when(core == h)
+                    def _():
+                        for event in mine:
+                            event()
+            if r == 1:
+                if q == 0:
+                    load_gate.wait()
+                lax.fori_loop(count * q // slots, count * (q + 1) // slots, silu_gate, 0)
+            elif waiting:
+                conv_pair(*waiting.pop(0))
+        if r == 1:
+            load_x.wait()
+            halo.wait_recv()
+        waiting += [(m, p) for m in groups[r - 1] for p in range(ny // 2)]
     hand_over(0)
+    for m, p in waiting:
+        conv_pair(m, p)
 
     low = proj_ref[:rank]
     mean = jnp.mean(low * low, axis=0, keepdims=True)
@@ -476,10 +497,10 @@
         step_kin(m, 1)
         return carry
 
-    lax.fori_loop(0, nz // 2, later_kin, 0)
+    lax.fori_loop(0, nz // 2 + 2, later_kin, 0)
     spread(c_ref, proj_ref[rank + states :])
     pl.when(lax.rem(y, 2) == 0)(prefix)
-    lax.fori_loop(nz // 2, nz, later_kin, 0)
+    lax.fori_loop(nz // 2 + 2, nz, later_kin, 0)
     send_ends(nz - 1, 1)
 
     def out_copy(s):
@@ -534,9 +555,9 @@
         return carry
 
     pairs = count // 2
-    lax.fori_loop(0, 3, scan_pair, 0)
+    lax.fori_loop(0, 4, scan_pair, 0)
     pl.when(lax.rem(y, 2) == 1)(prefix)
-    lax.fori_loop(3, pairs, scan_pair, 0)
+    lax.fori_loop(4, pairs, scan_pair, 0)
     both(lambda r: r.drain())
     halo.wait_send()
 

time: 96.3 us -> 92 us (0.955)
  Pallas kernels: 93.1 us -> 88.7 us
    pallas_call x1, Pallas kernels: 93.1 us -> 88.7 us  [local(): pl.pallas_call(functools.partial(mixer_kernel, ny, nz), in_specs=[hbm, hb...]
where the time goes in v4:
time: 92 us; the launch traced here: 91.8 us
  Pallas kernels  88.7 us (96%)
  local copies, waits for them, and re-layouts  3.1 us (3%)
    pallas_call x1, Pallas kernels, local(): pl.pallas_call(functools.partial(mixer_kernel, ny, nz), in_specs=[hbm, hb...  88.7 us
    unnamed x1, local copies, waits for them, and re-layouts  3.1 us

profile of v4, /device:TPU:8, one launch (start us, length us, event | category | flops | bytes accessed | tf_op | source)
XLA Modules:
  0.0 91.8 jit_solution(16163444443347765931)
XLA Ops:
  0.0 88.7 %mixer.1 = bf16[128,8192]{1,0:T(8,128)(2,1)} custom-call(bf16[128,8192]{1,0:T(8,128)(2,1)} %x_hbm.1, bf16[128,8192]{1,0:T(8,128)(2,1)} %gate_hbm.1, bf16[4,256]{1,0:T(4,128)(2,1)} %cw_ref.1, bf16[256]{0:T(256)(128)(2,1)} %cb_ref.1, bf16[288,256]{1,0:T(8,128)(2,1)} %bitcast.4, f32[1,256]{1,0:T(1,128)} %bitcast.5, bf16[256,256]{1,0:T(8,128)(2,1)} %dtw_ref.1, ...), custom_call_target="tpu_custom_call" | custom-call | tf_op jit(solution)/shard_map/mixer/pallas_call | solution.py:609
  88.7 3.1 %copy.12 = bf16[128,8192]{1,0:T(8,128)(2,1)} copy(bf16[128,8192]{1,0:T(8,128)(2,1)} %mixer.1) | data formatting | bytes 4194304
